TPU v7x, 512 devices: a whole 4x4x16 slice. The times are simulated.
512 devices in a mesh: lat: 16 (over y, z_lo), lon: 32 (over x, z_hi, core).
Axes of the slice: x: 4, y: 4, z: 16 (z_hi: 4, z_lo: 4; z = z_hi * 4 + z_lo), core: 2. Of those that a mesh axis runs over, the one named last changes fastest.
Arguments:
- atmos_patch_tokens: bfloat16 [256, 768, 512], P('lat', 'lon'), may hold values from -6 to 6
- atmos_norm_gain: float32 [512], replicated, may hold values from 0.5 to 1.5
- query_key_value_weight: bfloat16 [512, 1536], replicated, may hold values from -0.25 to 0.25
- query_key_value_bias: float32 [1536], replicated, may hold values from -3 to 3
- relative_bias_grid: float32 [16, 225], replicated, may hold values from -260 to 260
- attention_output_weight: bfloat16 [512, 512], replicated, may hold values from -0.25 to 0.25
- flux_projector: bfloat16 [512, 16], replicated, may hold values from -0.25 to 0.25
- surface_encoder: float32 [4, 512], replicated, may hold values from -1.5 to 1.5
- ocean_cell_state: bfloat16 [256, 1024, 256], P('lat', 'lon'), may hold values from -6 to 6
- land_sea_mask: int32 [256, 1024], P('lat', 'lon'), may hold values 0 or 1
- depthwise_conv_kernel: float32 [7, 7, 256], replicated, may hold values from -0.875 to 0.875
- depthwise_conv_bias: float32 [256], replicated, may hold values from -3 to 3
- ocean_norm_gain: float32 [256], replicated, may hold values from 0.5 to 1.5
- pointwise_expand: bfloat16 [256, 1024], replicated, may hold values from -0.375 to 0.375
- pointwise_contract: bfloat16 [1024, 256], replicated, may hold values from -0.1875 to 0.1875
- layer_update_scale: float32 [256], replicated, may hold values from 0.3 to 1.5
- forcing_encoder: float32 [16, 256], replicated, may hold values from -1.5 to 1.5
- surface_projector: float32 [256, 4], replicated, may hold values from -0.375 to 0.375
- overlay_area_weight: bfloat16 [16, 32, 3, 64, 512], P('lat', 'lon'), may hold values from 0 to 1, as said below
- owners: int32 [16, 32, 3], P('lat', 'lon'), may hold values from 0 to 31, as said below
- owner_tile_blocks: int32 [16, 32, 3], P('lat', 'lon'), may hold values from 0 to 5
- counts: int32 [16, 32], P('lat', 'lon'), may hold values from 1 to 3
Outputs:
- atm_out: bfloat16 [256, 768, 512], P('lat', 'lon')
- ocean_out: bfloat16 [256, 1024, 256], P('lat', 'lon')
Inputs may be any that keep to these rules, and one draw needn't show every extreme that they name: `overlay_area_weight`: nonnegative. `owners`: each slot's owner is the ocean tile's own longitude strip or one of the two beside it, cyclically. `owner_tile_blocks`: values of unused slots are arbitrary within the range.
All inputs are finite; a program needn't handle non-finite values. No bound on the sum of `land_sea_mask` on one device may be relied on, other than what follows from the above.
Results may differ from a plain program's by a relative error of at most 0.008.
Values may be sent and summed in bfloat16 or wider, within the bound.
A program may use at most 64 MiB of HBM per device.

v0:
```python
import jax
import jax.numpy as jnp
from jax import lax
from jax.sharding import PartitionSpec as P

HEADS = 16
WIN = 8
SHIFT = 4
BLK = 64
KER = 7


FULL_PRECISION = lax.Precision.HIGHEST


def passed_along(block, axis, distance):
    devices = range(lax.axis_size(axis))
    route = [((i - distance) % len(devices), i) for i in devices]
    return lax.ppermute(block, axis, route)


def extended(block, sides, width):
    for axis, dim in sides:
        count = lax.axis_size(axis)
        forward = [(i, i + 1) for i in range(count - 1)]
        forward.append((count - 1, 0))
        backward = [(target, source) for source, target in forward]
        low = lax.ppermute(
            lax.slice_in_dim(block, block.shape[dim] - width, None, axis=dim), axis, forward
        )
        high = lax.ppermute(lax.slice_in_dim(block, 0, width, axis=dim), axis, backward)
        block = jnp.concatenate([low, block, high], axis=dim)
    return block


def layer_norm(values, gain_vector, epsilon):
    average = jnp.mean(values, axis=-1, keepdims=True)
    centred = values - average
    spread = jnp.mean(centred * centred, axis=-1, keepdims=True)
    return centred * lax.rsqrt(spread + epsilon) * gain_vector


def to_windows(values, window):
    row_count, col_count, channel_total = values.shape
    pieces = values.reshape(
        row_count // window, window, col_count // window, window, channel_total
    ).transpose(0, 2, 1, 3, 4)
    return pieces.reshape(-1, window * window, channel_total)


def from_windows(values, row_count, col_count, window):
    channel_total = values.shape[-1]
    pieces = values.reshape(
        row_count // window, col_count // window, window, window, channel_total
    ).transpose(0, 2, 1, 3, 4)
    return pieces.reshape(row_count, col_count, channel_total)


def position_bias(lookup, window):
    places = jnp.arange(window * window, dtype=jnp.int32)
    row_place = places // window
    col_place = places % window
    offsets = (row_place[:, None] - row_place[None, :] + window - 1) * (2 * window - 1) + (
        col_place[:, None] - col_place[None, :] + window - 1
    )
    onehot = (
        offsets[:, :, None] == jnp.arange((2 * window - 1) ** 2, dtype=jnp.int32)[None, None, :]
    ).astype(jnp.float32)
    return jnp.einsum("hp,abp->hab", lookup, onehot, precision=FULL_PRECISION)


def window_attention(
    normed,
    region,
    query_key_value_weight,
    query_key_value_bias,
    pos_bias,
    attention_output_weight,
    head_count,
    window,
):
    row_count, col_count, feature_width = normed.shape
    head_size = feature_width // head_count
    qkv = (
        jnp.dot(
            normed.reshape(row_count * col_count, feature_width),
            query_key_value_weight,
            preferred_element_type=jnp.float32,
        )
        + query_key_value_bias
    )
    queries = (qkv[:, :feature_width] * head_size ** (-0.5)).astype(jnp.bfloat16)
    key_rows = qkv[:, feature_width : 2 * feature_width].astype(jnp.bfloat16)
    value_rows = qkv[:, 2 * feature_width :].astype(jnp.bfloat16)

    def split_heads(matrix):
        return to_windows(matrix.reshape(row_count, col_count, feature_width), window).reshape(
            -1, window * window, head_count, head_size
        )

    queries = split_heads(queries)
    key_rows = split_heads(key_rows)
    value_rows = split_heads(value_rows)
    labels = to_windows(region.reshape(row_count, col_count, 1), window)[:, :, 0]
    scores = (
        jnp.einsum("wahd,wbhd->whab", queries, key_rows, preferred_element_type=jnp.float32)
        + pos_bias[None]
    )
    same_region = labels[:, None, :, None] == labels[:, None, None, :]
    scores = jnp.where(same_region, scores, -1000000000.0)
    largest = jnp.max(scores, axis=-1, keepdims=True)
    expo = jnp.exp(scores - largest)
    weights = (expo / jnp.sum(expo, axis=-1, keepdims=True)).astype(jnp.bfloat16)
    attended = jnp.einsum(
        "whab,wbhd->wahd", weights, value_rows, preferred_element_type=jnp.float32
    ).astype(jnp.bfloat16)
    attended = from_windows(
        attended.reshape(-1, window * window, feature_width), row_count, col_count, window
    )
    attended = attended.reshape(row_count * col_count, feature_width)
    projected = jnp.dot(
        attended, attention_output_weight, preferred_element_type=jnp.float32
    ).astype(jnp.bfloat16)
    return projected.reshape(row_count, col_count, feature_width)


def local(
    atmos_patch_tokens,
    atmos_norm_gain,
    query_key_value_weight,
    query_key_value_bias,
    relative_bias_grid,
    attention_output_weight,
    flux_projector,
    surface_encoder,
    ocean_cell_state,
    land_sea_mask,
    depthwise_conv_kernel,
    depthwise_conv_bias,
    ocean_norm_gain,
    pointwise_expand,
    pointwise_contract,
    layer_update_scale,
    forcing_encoder,
    surface_projector,
    overlay_area_weight,
    owners,
    owner_tile_blocks,
    counts,
):
    lat_place = lax.axis_index("lat")
    lon_place = lax.axis_index("lon")
    lat_size = lax.axis_size("lat")
    lon_size = lax.axis_size("lon")
    tile_row_count, tile_columns, feature_width = atmos_patch_tokens.shape
    ocean_rows, ocean_cols, channel_total = ocean_cell_state.shape
    ocean_cell_grid = ocean_rows * ocean_cols
    block_count = tile_row_count * tile_columns // BLK
    slot_count = owners.shape[2]
    wet_cell_mask = land_sea_mask.astype(jnp.float32).reshape(ocean_cell_grid, 1)
    in_use = (jnp.arange(slot_count, dtype=jnp.int32) < counts[0, 0]).astype(jnp.float32)
    relative = (owners[0, 0] - lon_place + 1 + lon_size) % lon_size
    side_hot = (relative[:, None] == jnp.arange(3, dtype=jnp.int32)[None, :]).astype(
        jnp.float32
    ) * in_use[:, None]
    block_hot = (
        owner_tile_blocks[0, 0][:, None] == jnp.arange(block_count, dtype=jnp.int32)[None, :]
    ).astype(jnp.float32)
    ocean_mask_float = ocean_cell_state.astype(jnp.float32)
    regrid = overlay_area_weight[0, 0]
    surface_values = (
        jnp.dot(
            ocean_mask_float.reshape(ocean_cell_grid, channel_total),
            surface_projector,
            precision=FULL_PRECISION,
        )
        * wet_cell_mask
    ).astype(jnp.bfloat16)
    contrib = jnp.einsum("ktc,cs->kts", regrid, surface_values, preferred_element_type=jnp.float32)
    linear_apply = jnp.einsum(
        "ko,kb,kts->obts", side_hot, block_hot, contrib, precision=FULL_PRECISION
    )
    eastern_incoming = passed_along(linear_apply[0], "lon", -1)
    western_incoming = passed_along(linear_apply[2], "lon", 1)
    sea_surface_atmos = (linear_apply[1] + eastern_incoming + western_incoming).reshape(
        tile_row_count * tile_columns, -1
    )
    spatial_mixed = (
        atmos_patch_tokens.astype(jnp.float32)
        + jnp.dot(sea_surface_atmos, surface_encoder, precision=FULL_PRECISION).reshape(
            tile_row_count, tile_columns, feature_width
        )
    ).astype(jnp.bfloat16)
    normed = layer_norm(spatial_mixed.astype(jnp.float32), atmos_norm_gain, 1e-05).astype(
        jnp.bfloat16
    )
    pos_bias = position_bias(relative_bias_grid, WIN)
    rows_total = tile_row_count * lat_size
    incoming = passed_along(normed[:SHIFT], "lat", -1)
    rolled = jnp.concatenate([normed[SHIFT:], incoming], axis=0)
    incoming = passed_along(rolled[:, :SHIFT], "lon", -1)
    rolled = jnp.concatenate([rolled[:, SHIFT:], incoming], axis=1)
    global_rows = lat_place * tile_row_count + jnp.arange(tile_row_count, dtype=jnp.int32)
    region = (global_rows >= rows_total - SHIFT).astype(jnp.int32)
    region = jnp.broadcast_to(region[:, None], (tile_row_count, tile_columns))
    projected = window_attention(
        rolled,
        region,
        query_key_value_weight,
        query_key_value_bias,
        pos_bias,
        attention_output_weight,
        HEADS,
        WIN,
    )
    incoming = passed_along(projected[:, tile_columns - SHIFT :], "lon", 1)
    back = jnp.concatenate([incoming, projected[:, : tile_columns - SHIFT]], axis=1)
    incoming = passed_along(back[tile_row_count - SHIFT :], "lat", 1)
    back = jnp.concatenate([incoming, back[: tile_row_count - SHIFT]], axis=0)
    atm_out = (spatial_mixed.astype(jnp.float32) + back.astype(jnp.float32)).astype(jnp.bfloat16)
    flux = jnp.dot(
        atm_out.reshape(tile_row_count * tile_columns, feature_width),
        flux_projector,
        preferred_element_type=jnp.float32,
    ).astype(jnp.bfloat16)
    flux = flux.reshape(block_count, BLK, -1)
    beside_all = extended(flux[None], (("lon", 0),), 1)
    picked = jnp.einsum(
        "ko,kb,obtf->ktf",
        side_hot,
        block_hot,
        beside_all.astype(jnp.float32),
        precision=FULL_PRECISION,
    )
    forcing = jnp.einsum(
        "ktc,ktf->cf", regrid, picked.astype(jnp.bfloat16), preferred_element_type=jnp.float32
    )
    half = KER // 2
    padded = extended(ocean_cell_state, (("lat", 0), ("lon", 1)), half)
    padded_rows = lat_place * ocean_rows - half + jnp.arange(ocean_rows + 2 * half, dtype=jnp.int32)
    inside = (padded_rows >= 0) & (padded_rows < ocean_rows * lat_size)
    padded = jnp.where(inside[:, None, None], padded.astype(jnp.float32), 0.0)
    conv = jnp.zeros_like(ocean_mask_float) + depthwise_conv_bias
    for row_off in range(KER):
        for col_off in range(KER):
            conv = (
                conv
                + depthwise_conv_kernel[row_off, col_off]
                * padded[row_off : row_off + ocean_rows, col_off : col_off + ocean_cols]
            )
    pre = conv.reshape(ocean_cell_grid, channel_total) + jnp.dot(
        forcing, forcing_encoder, precision=FULL_PRECISION
    )
    ocean_normed = layer_norm(pre, ocean_norm_gain, 1e-06).astype(jnp.bfloat16)
    hidden = jax.nn.gelu(
        jnp.dot(ocean_normed, pointwise_expand, preferred_element_type=jnp.float32),
        approximate=False,
    ).astype(jnp.bfloat16)
    update = jnp.dot(hidden, pointwise_contract, preferred_element_type=jnp.float32)
    ocean_out = (
        ocean_mask_float.reshape(ocean_cell_grid, channel_total)
        + wet_cell_mask * layer_update_scale * update
    ).astype(jnp.bfloat16)
    return (atm_out, ocean_out.reshape(ocean_rows, ocean_cols, channel_total))


def solution(mesh):
    placed = (
        P("lat", "lon", None),
        P(),
        P(),
        P(),
        P(),
        P(),
        P(),
        P(),
        P("lat", "lon", None),
        P("lat", "lon"),
        P(),
        P(),
        P(),
        P(),
        P(),
        P(),
        P(),
        P(),
        P("lat", "lon", None, None, None),
        P("lat", "lon", None),
        P("lat", "lon", None),
        P("lat", "lon"),
    )
    return jax.shard_map(
        local,
        mesh=mesh,
        in_specs=placed,
        out_specs=(P("lat", "lon", None), P("lat", "lon", None)),
        check_vma=False,
    )
```

profile of v0, /device:TPU:8, one launch (start us, length us, event | category | flops | bytes accessed | tf_op | source)
XLA Modules:
  0.0 136.9 jit_solution(12545798736265013531)
XLA Ops:
  3.0 1.3 fusion.34
  6.4 14.4 %collective-permute-start = (f32[6,64,4]{1,0,2:T(8,128)S(1)}, f32[6,64,4]{1,0,2:T(8,128)S(1)}, u32[]{:S(2)}, u32[]{:S(2)}) collective-permute-start(f32[6,64,4]{1,0,2:T(8,128)S(1)} %get-tuple-element.57), channel_id=1, source_target_pairs={{1,0},{2,1},{3,2},{4,3},{5,4},{6,5},{7,6},{8,7},{9,8},{10,9},{11,1... | collective-permute-start | bytes 18440 | tf_op jit(solution)/shard_map/ppermute | solution.py:19
  20.8 1.9 %collective-permute-start.1 = (f32[6,64,4]{1,0,2:T(8,128)S(1)}, f32[6,64,4]{1,0,2:T(8,128)S(1)}, u32[]{:S(2)}, u32[]{:S(2)}) collective-permute-start(f32[6,64,4]{1,0,2:T(8,128)S(1)} %get-tuple-element.58), channel_id=1, source_target_pairs={{31,0},{0,1},{1,2},{2,3},{3,4},{4,5},{5,6},{6,7},{7,8},{8,9},{9,10... | collective-permute-start | bytes 18440 | tf_op jit(solution)/shard_map/ppermute | solution.py:19
  23.6 2.9 %collective-permute-start.6 = (bf16[3,32,256]{2,1,0:T(8,128)(2,1)S(1)}, bf16[3,32,256]{2,1,0:T(8,128)(2,1)S(1)}, u32[]{:S(2)}, u32[]{:S(2)}) collective-permute-start(bf16[3,32,256]{2,1,0:T(8,128)(2,1)S(1)} %get-tuple-element.7), channel_id=1, source_target_pairs={{0,32},{32,64},{64,96},{96,128},{128,160},{160,192},{192,224},{224... | collective-permute-start | bytes 147464 | tf_op jit(solution)/shard_map/ppermute | solution.py:28
  26.5 5.6 %collective-permute-start.7 = (bf16[3,32,256]{2,1,0:T(8,128)(2,1)S(1)}, bf16[3,32,256]{2,1,0:T(8,128)(2,1)S(1)}, u32[]{:S(2)}, u32[]{:S(2)}) collective-permute-start(bf16[3,32,256]{2,1,0:T(8,128)(2,1)S(1)} %get-tuple-element.6), channel_id=1, source_target_pairs={{32,0},{64,32},{96,64},{128,96},{160,128},{192,160},{224,192},{256... | collective-permute-start | bytes 147464 | tf_op jit(solution)/shard_map/ppermute | solution.py:31
  32.1 1.6 %fusion.183 = (f32[1,1,256]{2,1,0:T(1,128)S(1)}, f32[1,1,256]{2,1,0:T(1,128)S(1)}, f32[1,1,256]{2,1,0:T(1,128)S(1)}, f32[1,1,256]{2,1,0:T(1,128)S(1)}, f32[1,1,2...) fusion(f32[7,7,256]{2,1,0:T(8,128)} %param.32), kind=kLoop, calls=%fused_computation.289 | loop fusion | bytes 38912 | tf_op jit(solution)/shard_map/slice | solution.py:248
  33.7 1.7 %fusion.184 = (f32[1,1,256]{2,1,0:T(1,128)}, f32[1,1,256]{2,1,0:T(1,128)}, f32[1,1,256]{2,1,0:T(1,128)}, f32[1,1,256]{2,1,0:T(1,128)}, f32[1,1,256]{2,1,0:T(1,12...) fusion(f32[7,7,256]{2,1,0:T(8,128)} %param.32), kind=kLoop, calls=%fused_computation.290 | loop fusion | bytes 38912 | tf_op jit(solution)/shard_map/slice | solution.py:248
  35.4 1.5 %fusion.185 = (f32[1,1,256]{2,1,0:T(1,128)}, f32[1,1,256]{2,1,0:T(1,128)}, f32[1,1,256]{2,1,0:T(1,128)}, f32[1,1,256]{2,1,0:T(1,128)}, f32[1,1,256]{2,1,0:T(1,12...) fusion(f32[7,7,256]{2,1,0:T(8,128)} %param.32), kind=kLoop, calls=%fused_computation.291 | loop fusion | bytes 22528 | tf_op jit(solution)/shard_map/slice | solution.py:248
  37.3 3.3 %fusion.30 = f32[16,64,64]{2,0,1:T(8,128)S(1)} fusion(s32[64,64]{1,0:T(8,128)S(1)} %add_add_fusion, f32[16,225]{1,0:T(8,128)} %param.26), kind=kOutput, calls=%fused_computation.42 | convolution fusion | flops 177868800 | bytes 292928 | tf_op jit(solution)/shard_map/hp,abp->hab/dot_general | solution.py:69
  42.4 1.9 %fusion.186 = (f32[16,24]{1,0:T(8,128)S(1)}, f32[16,24,512]{2,1,0:T(8,128)S(1)}) fusion(f32[4,512]{1,0:T(4,128)S(1)} %copy-done.11, f32[16,24,4]{1,0,2:T(8,128)S(1)} %dot_general.66, bf16[16,24,512]{2,1,0:T(8,128)(2,1)} %param.22), kind=kOutput, calls=%fused_computation.292 | convolution fusion | flops 10419840 | bytes 1195520 | tf_op jit(solution)/shard_map/dot_general | solution.py:190
  44.9 1.9 %collective-permute-start.2 = (bf16[4,24,512]{2,1,0:T(8,128)(2,1)S(1)}, bf16[4,24,512]{2,1,0:T(8,128)(2,1)S(1)}, u32[]{:S(2)}, u32[]{:S(2)}) collective-permute-start(bf16[4,24,512]{2,1,0:T(8,128)(2,1)S(1)} %slice.470), channel_id=1, source_target_pairs={{32,0},{64,32},{96,64},{128,96},{160,128},{192,160},{224,192},{256... | collective-permute-start | bytes 294920 | tf_op jit(solution)/shard_map/ppermute | solution.py:19
  46.9 4.5 %collective-permute-done.2 = bf16[4,24,512]{2,1,0:T(8,128)(2,1)S(1)} collective-permute-done((bf16[4,24,512]{2,1,0:T(8,128)(2,1)S(1)}, bf16[4,24,512]{2,1,0:T(8,128)(2,1)S(1)}, u32[]{:S(2)}, u32[]{:S(2)}) %collective-permute-start.2) | collective-permute-done | bytes 98336 | tf_op jit(solution)/shard_map/ppermute | solution.py:19
  51.4 8.1 %collective-permute-start.3 = (bf16[16,4,512]{2,1,0:T(4,128)(2,1)S(1)}, bf16[16,4,512]{2,1,0:T(4,128)(2,1)S(1)}, u32[]{:S(2)}, u32[]{:S(2)}) collective-permute-start(bf16[16,4,512]{2,1,0:T(4,128)(2,1)S(1)} %pad_maximum_fusion.3), channel_id=1, source_target_pairs={{1,0},{2,1},{3,2},{4,3},{5,4},{6,5},{7,6},{8,7},{9,8},{10,9},{11,1... | collective-permute-start | bytes 196616 | tf_op jit(solution)/shard_map/ppermute | solution.py:19
  59.7 1.6 %collective-permute-done.3 = bf16[16,4,512]{2,1,0:T(4,128)(2,1)S(1)} collective-permute-done((bf16[16,4,512]{2,1,0:T(4,128)(2,1)S(1)}, bf16[16,4,512]{2,1,0:T(4,128)(2,1)S(1)}, u32[]{:S(2)}, u32[]{:S(2)}) %collective-permute-start.3) | collective-permute-done | bytes 65568 | tf_op jit(solution)/shard_map/ppermute | solution.py:19
  61.3 2.2 %fusion.187 = (bf16[384,1536]{1,0:T(8,128)(2,1)S(1)}, f32[384,1536]{1,0:T(8,128)}) fusion(f32[1536]{0:T(1024)S(1)} %copy-done.8, bf16[384,512]{1,0:T(8,128)(2,1)S(1)} %bitcast.157, bf16[512,1536]{1,0:T(8,128)(2,1)S(1)} %copy-done), kind=kOutput, calls=%fused_computation.293 | convolution fusion | flops 605159424 | bytes 5511168 | tf_op jit(solution)/shard_map/dot_general | solution.py:85
  64.4 2.9 %reshape_reshape.30 = bf16[6,64,16,32]{3,2,1,0:T(8,128)(2,1)} reshape(bf16[2,3,8,8,512]{4,3,2,1,0:T(8,128)(2,1)} %bitcast.164) | data formatting | bytes 786432 | tf_op jit(solution)/shard_map/reshape;reshape | solution.py:97
  67.3 1.2 fusion.65
  69.2 2.9 %reshape_reshape.28 = bf16[6,64,16,32]{3,2,1,0:T(8,128)(2,1)} reshape(bf16[2,3,8,8,512]{4,3,2,1,0:T(8,128)(2,1)} %bitcast.165) | data formatting | bytes 786432 | tf_op jit(solution)/shard_map/reshape;reshape | solution.py:97
  72.2 2.0 %reshape_reshape.26 = bf16[6,64,16,32]{3,2,1,0:T(8,128)(2,1)} reshape(bf16[2,3,8,8,512]{4,3,2,1,0:T(8,128)(2,1)S(1)} %bitcast.166) | data formatting | bytes 786432 | tf_op jit(solution)/shard_map/reshape;reshape | solution.py:97
  74.2 2.9 %fusion.16 = f32[6,16,64,64]{2,3,1,0:T(8,128)S(1)} fusion(bf16[6,64,16,32]{3,2,1,0:T(8,128)(2,1)} %reshape_reshape.30, bf16[6,64,16,32]{3,2,1,0:T(8,128)(2,1)} %reshape_reshape.28), kind=kOutput, calls=%fused_computation.30 | convolution fusion | flops 25165824 | bytes 2359296 | tf_op jit(solution)/shard_map/wahd,wbhd->whab/dot_general | solution.py:106
  79.1 2.1 %copy.40 = bf16[6,64,16,32]{3,2,1,0:T(8,128)(2,1)} copy(bf16[6,64,16,32]{1,3,2,0:T(8,128)(2,1)S(1)} %fusion.25) | data formatting | bytes 786432 | tf_op jit(solution)/shard_map/convert_element_type | solution.py:116
  81.2 2.7 %reshape_reshape.31 = bf16[2,3,8,8,512]{4,3,2,1,0:T(8,128)(2,1)S(1)} reshape(bf16[6,64,16,32]{3,2,1,0:T(8,128)(2,1)} %copy.40) | data formatting | bytes 786432 | tf_op jit(solution)/shard_map/reshape;reshape | solution.py:53
  84.0 1.4 %convolution_convert_fusion = bf16[384,512]{1,0:T(8,128)(2,1)S(1)} fusion(bf16[384,512]{1,0:T(8,128)(2,1)S(1)} %bitcast.163, bf16[512,512]{1,0:T(8,128)(2,1)} %param.27), kind=kOutput, calls=%fused_computation.39 | convolution fusion | flops 201523200 | bytes 1310720 | tf_op jit(solution)/shard_map/dot_general | solution.py:121
  85.5 1.9 %collective-permute-start.4 = (bf16[16,4,512]{2,1,0:T(4,128)(2,1)S(1)}, bf16[16,4,512]{2,1,0:T(4,128)(2,1)S(1)}, u32[]{:S(2)}, u32[]{:S(2)}) collective-permute-start(bf16[16,4,512]{2,1,0:T(4,128)(2,1)S(1)} %slice.476), channel_id=1, source_target_pairs={{31,0},{0,1},{1,2},{2,3},{3,4},{4,5},{5,6},{6,7},{7,8},{8,9},{9,10... | collective-permute-start | bytes 196616 | tf_op jit(solution)/shard_map/ppermute | solution.py:19
  88.4 1.9 %collective-permute-start.8 = (bf16[22,3,256]{2,1,0:T(4,128)(2,1)S(1)}, bf16[22,3,256]{2,1,0:T(4,128)(2,1)S(1)}, u32[]{:S(2)}, u32[]{:S(2)}) collective-permute-start(bf16[22,3,256]{2,1,0:T(4,128)(2,1)S(1)} %get-tuple-element.4), channel_id=1, source_target_pairs={{0,1},{1,2},{2,3},{3,4},{4,5},{5,6},{6,7},{7,8},{8,9},{9,10},{10,1... | collective-permute-start | bytes 101384 | tf_op jit(solution)/shard_map/ppermute | solution.py:28
  90.3 9.8 %collective-permute-start.9 = (bf16[22,3,256]{2,1,0:T(4,128)(2,1)S(1)}, bf16[22,3,256]{2,1,0:T(4,128)(2,1)S(1)}, u32[]{:S(2)}, u32[]{:S(2)}) collective-permute-start(bf16[22,3,256]{2,1,0:T(4,128)(2,1)S(1)} %get-tuple-element.5), channel_id=1, source_target_pairs={{1,0},{2,1},{3,2},{4,3},{5,4},{6,5},{7,6},{8,7},{9,8},{10,9},{11,1... | collective-permute-start | bytes 101384 | tf_op jit(solution)/shard_map/ppermute | solution.py:31
  100.2 1.9 %collective-permute-start.5 = (bf16[4,24,512]{2,1,0:T(8,128)(2,1)S(1)}, bf16[4,24,512]{2,1,0:T(8,128)(2,1)S(1)}, u32[]{:S(2)}, u32[]{:S(2)}) collective-permute-start(bf16[4,24,512]{2,1,0:T(8,128)(2,1)S(1)} %pad_maximum_fusion.2), channel_id=1, source_target_pairs={{480,0},{0,32},{32,64},{64,96},{96,128},{128,160},{160,192},{192,2... | collective-permute-start | bytes 294920 | tf_op jit(solution)/shard_map/ppermute | solution.py:19
  102.4 7.1 %collective-permute-done.5 = bf16[4,24,512]{2,1,0:T(8,128)(2,1)S(1)} collective-permute-done((bf16[4,24,512]{2,1,0:T(8,128)(2,1)S(1)}, bf16[4,24,512]{2,1,0:T(8,128)(2,1)S(1)}, u32[]{:S(2)}, u32[]{:S(2)}) %collective-permute-start.5) | collective-permute-done | bytes 98336 | tf_op jit(solution)/shard_map/ppermute | solution.py:19
  110.7 1.9 %collective-permute-start.10 = (bf16[1,6,64,16]{2,1,3,0:T(8,128)(2,1)S(1)}, bf16[1,6,64,16]{2,1,3,0:T(8,128)(2,1)}, u32[]{:S(2)}, u32[]{:S(2)}) collective-permute-start(bf16[1,6,64,16]{2,1,3,0:T(8,128)(2,1)S(1)} %broadcast_in_dim_reshape.3), channel_id=1, source_target_pairs={{0,1},{1,2},{2,3},{3,4},{4,5},{5,6},{6,7},{7,8},{8,9},{9,10},{10,1... | collective-permute-start | bytes 36872 | tf_op jit(solution)/shard_map/ppermute | solution.py:28
  112.6 9.9 %collective-permute-start.11 = (bf16[1,6,64,16]{2,1,3,0:T(8,128)(2,1)S(1)}, bf16[1,6,64,16]{2,1,3,0:T(8,128)(2,1)}, u32[]{:S(2)}, u32[]{:S(2)}) collective-permute-start(bf16[1,6,64,16]{2,1,3,0:T(8,128)(2,1)S(1)} %broadcast_in_dim_reshape.3), channel_id=1, source_target_pairs={{1,0},{2,1},{3,2},{4,3},{5,4},{6,5},{7,6},{8,7},{9,8},{10,9},{11,1... | collective-permute-start | bytes 36872 | tf_op jit(solution)/shard_map/ppermute | solution.py:31
  122.6 4.9 %fusion.66 = f32[16,32,256]{2,1,0:T(8,128)S(1)} fusion(f32[22,38,256]{2,1,0:T(8,128)S(1)} %convert_select_fusion, f32[256]{0:T(256)} %bitcast.217, f32[256]{0:T(256)} %bitcast.218, f32[256]{0:T(256)S(1)} %bitcast.171, f32[256]{0:T(256)S(1)} %bitcast.172, f32[256]{0:T(256)S(1)} %bitcast.173, f32[256]{0:T(256)S(1)} %bitcast.174, f32[256]{0:T(256)S(1)} %bitcast.175, ...), kind=kLoop, calls=%fused_computation.91 | loop fusion | flops 12845056 | bytes 26265600 | tf_op jit(solution)/shard_map/add | solution.py:247
  129.8 7.0 %fusion.32 = bf16[512,256]{1,0:T(8,128)(2,1)} fusion(bf16[1024,256]{1,0:T(8,128)(2,1)} %param.36, bf16[256,1024]{1,0:T(8,128)(2,1)} %param.35, bf16[512,256]{1,0:T(8,128)(2,1)S(1)} %bitcast.169, f32[512,256]{0,1:T(8,128)S(1)} %get-tuple-element.66, f32[256]{0:T(256)S(1)} %copy-done.20, f32[512]{0:T(512)S(1)} %add_rsqrt_fusion.1, ...), kind=kOutput, calls=%fused_computation.46 | convolution fusion | flops 572129280 | bytes 2105344 | tf_op jit(solution)/shard_map/dot_general | solution.py:259
  (107 shorter events, 15.9 us)
Async XLA Ops:
  0.6 60.7 %copy-start = (bf16[512,1536]{1,0:T(8,128)(2,1)S(1)}, bf16[512,1536]{1,0:T(8,128)(2,1)}, u32[]{:S(2)}) copy-start(bf16[512,1536]{1,0:T(8,128)(2,1)} %param.24) | copy-start | bytes 4718596
  0.6 41.8 %copy-start.11 = (f32[4,512]{1,0:T(4,128)S(1)}, f32[4,512]{1,0:T(4,128)}, u32[]{:S(2)}) copy-start(f32[4,512]{1,0:T(4,128)} %param.29) | copy-start | bytes 24580
  3.0 34.3 %copy-start.15 = (f32[3,6]{1,0:T(4,128)}, f32[3,6]{1,0:T(4,128)S(1)}, u32[]{:S(2)}) copy-start(f32[3,6]{1,0:T(4,128)S(1)} %fusion.145) | copy-start | bytes 220
  6.1 31.2 %copy-start.17 = (f32[3,3]{0,1:T(4,128)}, f32[3,3]{0,1:T(4,128)S(1)}, u32[]{:S(2)}) copy-start(f32[3,3]{0,1:T(4,128)S(1)} %fusion.146) | copy-start | bytes 112
  6.4 35.9 %collective-permute-start = (f32[6,64,4]{1,0,2:T(8,128)S(1)}, f32[6,64,4]{1,0,2:T(8,128)S(1)}, u32[]{:S(2)}, u32[]{:S(2)}) collective-permute-start(f32[6,64,4]{1,0,2:T(8,128)S(1)} %get-tuple-element.57), channel_id=1, source_target_pairs={{1,0},{2,1},{3,2},{4,3},{5,4},{6,5},{7,6},{8,7},{9,8},{10,9},{11,1... | collective-permute-start | bytes 18440 | tf_op jit(solution)/shard_map/ppermute | solution.py:19
  20.8 21.5 %collective-permute-start.1 = (f32[6,64,4]{1,0,2:T(8,128)S(1)}, f32[6,64,4]{1,0,2:T(8,128)S(1)}, u32[]{:S(2)}, u32[]{:S(2)}) collective-permute-start(f32[6,64,4]{1,0,2:T(8,128)S(1)} %get-tuple-element.58), channel_id=1, source_target_pairs={{31,0},{0,1},{1,2},{2,3},{3,4},{4,5},{5,6},{6,7},{7,8},{8,9},{9,10... | collective-permute-start | bytes 18440 | tf_op jit(solution)/shard_map/ppermute | solution.py:19
  23.6 23.2 %collective-permute-start.6 = (bf16[3,32,256]{2,1,0:T(8,128)(2,1)S(1)}, bf16[3,32,256]{2,1,0:T(8,128)(2,1)S(1)}, u32[]{:S(2)}, u32[]{:S(2)}) collective-permute-start(bf16[3,32,256]{2,1,0:T(8,128)(2,1)S(1)} %get-tuple-element.7), channel_id=1, source_target_pairs={{0,32},{32,64},{64,96},{96,128},{128,160},{160,192},{192,224},{224... | collective-permute-start | bytes 147464 | tf_op jit(solution)/shard_map/ppermute | solution.py:28
  26.5 20.4 %collective-permute-start.7 = (bf16[3,32,256]{2,1,0:T(8,128)(2,1)S(1)}, bf16[3,32,256]{2,1,0:T(8,128)(2,1)S(1)}, u32[]{:S(2)}, u32[]{:S(2)}) collective-permute-start(bf16[3,32,256]{2,1,0:T(8,128)(2,1)S(1)} %get-tuple-element.6), channel_id=1, source_target_pairs={{32,0},{64,32},{96,64},{128,96},{160,128},{192,160},{224,192},{256... | collective-permute-start | bytes 147464 | tf_op jit(solution)/shard_map/ppermute | solution.py:31
  40.7 3.9 %copy-start.14 = (f32[512]{0:T(512)S(1)}, f32[512]{0:T(512)}, u32[]{:S(2)}) copy-start(f32[512]{0:T(512)} %param.23) | copy-start | bytes 6148
  42.3 4.5 %copy-start.3 = (bf16[16,32,256]{2,1,0:T(8,128)(2,1)S(1)}, bf16[16,32,256]{2,1,0:T(8,128)(2,1)}, u32[]{:S(2)}) copy-start(bf16[16,32,256]{2,1,0:T(8,128)(2,1)} %param.30) | copy-start | bytes 786436
  44.8 16.5 %copy-start.8 = (f32[1536]{0:T(1024)S(1)}, f32[1536]{0:T(1024)}, u32[]{:S(2)}) copy-start(f32[1536]{0:T(1024)} %param.25) | copy-start | bytes 18436
  44.9 6.5 %collective-permute-start.2 = (bf16[4,24,512]{2,1,0:T(8,128)(2,1)S(1)}, bf16[4,24,512]{2,1,0:T(8,128)(2,1)S(1)}, u32[]{:S(2)}, u32[]{:S(2)}) collective-permute-start(bf16[4,24,512]{2,1,0:T(8,128)(2,1)S(1)} %slice.470), channel_id=1, source_target_pairs={{32,0},{64,32},{96,64},{128,96},{160,128},{192,160},{224,192},{256... | collective-permute-start | bytes 294920 | tf_op jit(solution)/shard_map/ppermute | solution.py:19
  46.9 4.5 %copy-start.5 = (bf16[22,32,256]{2,1,0:T(8,128)(2,1)}, bf16[22,32,256]{2,1,0:T(8,128)(2,1)S(1)}, u32[]{:S(2)}) copy-start(bf16[22,32,256]{2,1,0:T(8,128)(2,1)S(1)} %constant_dynamic-update-slice_fusion) | copy-start | bytes 1081348
  51.4 9.8 %collective-permute-start.3 = (bf16[16,4,512]{2,1,0:T(4,128)(2,1)S(1)}, bf16[16,4,512]{2,1,0:T(4,128)(2,1)S(1)}, u32[]{:S(2)}, u32[]{:S(2)}) collective-permute-start(bf16[16,4,512]{2,1,0:T(4,128)(2,1)S(1)} %pad_maximum_fusion.3), channel_id=1, source_target_pairs={{1,0},{2,1},{3,2},{4,3},{5,4},{6,5},{7,6},{8,7},{9,8},{10,9},{11,1... | collective-permute-start | bytes 196616 | tf_op jit(solution)/shard_map/ppermute | solution.py:19
  74.2 2.9 %copy-start.7 = (f32[16,64,64]{1,2,0:T(8,128)S(1)}, f32[16,64,64]{1,2,0:T(8,128)}, u32[]{:S(2)}) copy-start(f32[16,64,64]{1,2,0:T(8,128)} %copy.37) | copy-start | bytes 786436
  83.9 18.2 %copy-start.6 = (bf16[22,32,256]{2,1,0:T(8,128)(2,1)S(1)}, bf16[22,32,256]{2,1,0:T(8,128)(2,1)}, u32[]{:S(2)}) copy-start(bf16[22,32,256]{2,1,0:T(8,128)(2,1)} %copy-done.5) | copy-start | bytes 1081348
  84.0 18.2 %copy-start.19 = (pred[22]{0:T(512)(128)(4,1)S(1)}, pred[22]{0:T(512)(128)(4,1)}, u32[]{:S(2)}) copy-start(pred[22]{0:T(512)(128)(4,1)} %compare_and_fusion) | copy-start | bytes 70
  85.5 24.9 %copy-start.10 = (bf16[512,16]{0,1:T(8,128)(2,1)S(1)}, bf16[512,16]{0,1:T(8,128)(2,1)}, u32[]{:S(2)}) copy-start(bf16[512,16]{0,1:T(8,128)(2,1)} %param.28) | copy-start | bytes 49156
  85.5 14.6 %collective-permute-start.4 = (bf16[16,4,512]{2,1,0:T(4,128)(2,1)S(1)}, bf16[16,4,512]{2,1,0:T(4,128)(2,1)S(1)}, u32[]{:S(2)}, u32[]{:S(2)}) collective-permute-start(bf16[16,4,512]{2,1,0:T(4,128)(2,1)S(1)} %slice.476), channel_id=1, source_target_pairs={{31,0},{0,1},{1,2},{2,3},{3,4},{4,5},{5,6},{6,7},{7,8},{8,9},{9,10... | collective-permute-start | bytes 196616 | tf_op jit(solution)/shard_map/ppermute | solution.py:19
  88.4 13.7 %collective-permute-start.8 = (bf16[22,3,256]{2,1,0:T(4,128)(2,1)S(1)}, bf16[22,3,256]{2,1,0:T(4,128)(2,1)S(1)}, u32[]{:S(2)}, u32[]{:S(2)}) collective-permute-start(bf16[22,3,256]{2,1,0:T(4,128)(2,1)S(1)} %get-tuple-element.4), channel_id=1, source_target_pairs={{0,1},{1,2},{2,3},{3,4},{4,5},{5,6},{6,7},{7,8},{8,9},{9,10},{10,1... | collective-permute-start | bytes 101384 | tf_op jit(solution)/shard_map/ppermute | solution.py:28
  90.3 11.8 %collective-permute-start.9 = (bf16[22,3,256]{2,1,0:T(4,128)(2,1)S(1)}, bf16[22,3,256]{2,1,0:T(4,128)(2,1)S(1)}, u32[]{:S(2)}, u32[]{:S(2)}) collective-permute-start(bf16[22,3,256]{2,1,0:T(4,128)(2,1)S(1)} %get-tuple-element.5), channel_id=1, source_target_pairs={{1,0},{2,1},{3,2},{4,3},{5,4},{6,5},{7,6},{8,7},{9,8},{10,9},{11,1... | collective-permute-start | bytes 101384 | tf_op jit(solution)/shard_map/ppermute | solution.py:31
  100.1 22.3 %copy-start.12 = (f32[1,1,256]{2,1,0:T(1,128)S(1)}, f32[1,1,256]{2,1,0:T(1,128)}, u32[]{:S(2)}) copy-start(f32[1,1,256]{2,1,0:T(1,128)} %get-tuple-element.13) | copy-start | bytes 3076
  100.2 22.3 %copy-start.13 = (f32[1,1,256]{2,1,0:T(1,128)S(1)}, f32[1,1,256]{2,1,0:T(1,128)}, u32[]{:S(2)}) copy-start(f32[1,1,256]{2,1,0:T(1,128)} %get-tuple-element.14) | copy-start | bytes 3076
  100.2 9.2 %collective-permute-start.5 = (bf16[4,24,512]{2,1,0:T(8,128)(2,1)S(1)}, bf16[4,24,512]{2,1,0:T(8,128)(2,1)S(1)}, u32[]{:S(2)}, u32[]{:S(2)}) collective-permute-start(bf16[4,24,512]{2,1,0:T(8,128)(2,1)S(1)} %pad_maximum_fusion.2), channel_id=1, source_target_pairs={{480,0},{0,32},{32,64},{64,96},{96,128},{128,160},{160,192},{192,2... | collective-permute-start | bytes 294920 | tf_op jit(solution)/shard_map/ppermute | solution.py:19
  110.7 17.0 %collective-permute-start.10 = (bf16[1,6,64,16]{2,1,3,0:T(8,128)(2,1)S(1)}, bf16[1,6,64,16]{2,1,3,0:T(8,128)(2,1)}, u32[]{:S(2)}, u32[]{:S(2)}) collective-permute-start(bf16[1,6,64,16]{2,1,3,0:T(8,128)(2,1)S(1)} %broadcast_in_dim_reshape.3), channel_id=1, source_target_pairs={{0,1},{1,2},{2,3},{3,4},{4,5},{5,6},{6,7},{7,8},{8,9},{9,10},{10,1... | collective-permute-start | bytes 36872 | tf_op jit(solution)/shard_map/ppermute | solution.py:28
  112.6 15.1 %collective-permute-start.11 = (bf16[1,6,64,16]{2,1,3,0:T(8,128)(2,1)S(1)}, bf16[1,6,64,16]{2,1,3,0:T(8,128)(2,1)}, u32[]{:S(2)}, u32[]{:S(2)}) collective-permute-start(bf16[1,6,64,16]{2,1,3,0:T(8,128)(2,1)S(1)} %broadcast_in_dim_reshape.3), channel_id=1, source_target_pairs={{1,0},{2,1},{3,2},{4,3},{5,4},{6,5},{7,6},{8,7},{9,8},{10,9},{11,1... | collective-permute-start | bytes 36872 | tf_op jit(solution)/shard_map/ppermute | solution.py:31
  122.5 5.2 %copy-start.16 = (f32[3,6]{1,0:T(4,128)S(1)}, f32[3,6]{1,0:T(4,128)}, u32[]{:S(2)}) copy-start(f32[3,6]{1,0:T(4,128)} %copy-done.15) | copy-start | bytes 220
  122.5 5.2 %copy-start.18 = (f32[3,3]{0,1:T(4,128)S(1)}, f32[3,3]{0,1:T(4,128)}, u32[]{:S(2)}) copy-start(f32[3,3]{0,1:T(4,128)} %copy-done.17) | copy-start | bytes 112
  122.5 6.4 %copy-start.4 = (bf16[1,1,3,64,512]{4,3,2,1,0:T(8,128)(2,1)S(1)}, bf16[1,1,3,64,512]{4,3,2,1,0:T(8,128)(2,1)}, u32[]{:S(2)}) copy-start(bf16[1,1,3,64,512]{4,3,2,1,0:T(8,128)(2,1)} %param.40) | copy-start | bytes 589828
  122.5 6.5 %copy-start.9 = (f32[16,256]{1,0:T(8,128)S(1)}, f32[16,256]{1,0:T(8,128)}, u32[]{:S(2)}) copy-start(f32[16,256]{1,0:T(8,128)} %param.38) | copy-start | bytes 49156
  127.4 2.4 %copy-start.20 = (f32[256]{0:T(256)S(1)}, f32[256]{0:T(256)}, u32[]{:S(2)}) copy-start(f32[256]{0:T(256)} %param.34) | copy-start | bytes 3076
  127.4 2.4 %copy-start.21 = (f32[256]{0:T(256)S(1)}, f32[256]{0:T(256)}, u32[]{:S(2)}) copy-start(f32[256]{0:T(256)} %param.37) | copy-start | bytes 3076
  (2 other events, 2.2 us)
where the time goes:
time: 138 us; the launch traced here: 137 us
  starting transfers between devices  62.2 us (45%)
  matrix products  24.3 us (18%)
  local copies, waits for them, and re-layouts  24 us (17%)
  waiting for transfers between devices  13.2 us (10%)
  other arithmetic  11.2 us (8%)
  between operations  2.02 us (1%)
    ppermute x6, starting transfers between devices, passed_along(): return lax.ppermute(block, axis, route)  30.2 us
    ppermute x3, starting transfers between devices, extended(): lax.ppermute(lax.slice_in_dim(block, 0, width, axis=dim), axis, backward)  25.3 us
    ppermute x6, waiting for transfers between devices, passed_along(): return lax.ppermute(block, axis, route)  13.1 us
    another operation x3, local copies, waits for them, and re-layouts, split_heads(): to_windows(matrix.reshape(row_count, col_count, feature_width), window)  7.79 us
    dot_general x1, matrix products, local(): jnp.dot(hidden, pointwise_contract, preferred_element_type=jnp.float32)  7.02 us
    ppermute x3, starting transfers between devices, extended(): lax.ppermute(lax.slice_in_dim(block, block.shape[dim] - width, None, axis...  6.75 us
    add x1, other arithmetic, local(): conv + depthwise_conv_kernel[row_off, col_off] * padded[row_off:row_off +...  4.86 us
    slice x3, local copies, waits for them, and re-layouts, local(): depthwise_conv_kernel[row_off, col_off]  4.81 us
  transfers between devices with their start and end apart: 12, of which 3 were waited for; matrix products, arithmetic and copies ran while one was open for 14% of the time, Pallas kernels for 0%

commit v1 on v0

v1 whole, which is shorter than its diff:
```python
import functools

import jax
import jax.numpy as jnp
from jax import lax
from jax.experimental import pallas as pl
from jax.experimental.pallas import tpu as pltpu
from jax.sharding import PartitionSpec as P

F32 = jnp.float32
BF16 = jnp.bfloat16
MESH = pl.DeviceIdType.MESH
HEADS = 16
HALF = 8
WIN = 8
NT = (((1,), (1,)), ((), ()))
TN = (((0,), (0,)), ((), ()))
NN = (((1,), (0,)), ((), ()))


def dot(a, b, dims):
    return lax.dot_general(a, b, dims, preferred_element_type=F32)


def iota(shape, dim):
    return lax.broadcasted_iota(jnp.int32, shape, dim)


def low_half(shape):
    return iota(shape, len(shape) - 2) % 8 < 4


def turn(x):
    return pltpu.roll(x, 4, x.ndim - 2)


def pack(x, high):
    n, _, lanes = x.shape
    x = x.reshape(n // 2, 2, 8, lanes)
    even, odd = x[:, 0], x[:, 1]
    if high:
        even = turn(even)
    else:
        odd = turn(odd)
    return jnp.where(low_half(even.shape), even, odd)


def unpack(x, high):
    n, _, lanes = x.shape
    other = turn(x)
    pair = (other, x) if high else (x, other)
    return jnp.stack(pair, axis=1).reshape(2 * n, 8, lanes)


def split2(x):
    top = x.astype(BF16).astype(F32)
    return top, x - top


def split3(x):
    top, rest = split2(x)
    middle, last = split2(rest)
    return top, middle, last


def greet(partners):
    barrier = pltpu.get_barrier_semaphore()
    for device in partners:
        pl.semaphore_signal(barrier, inc=1, device_id=device, device_id_type=MESH)
    return lambda: pl.semaphore_wait(barrier, len(partners))


def place():
    la, lo = lax.axis_index("lat"), lax.axis_index("lon")
    nla, nlo = lax.axis_size("lat"), lax.axis_size("lon")
    return lambda di, dj: (lax.rem(la + di + nla, nla), lax.rem(lo + dj + nlo, nlo))


SURFACE_PARTNERS = [
    (di, dj) for di in (-1, 0, 1) for dj in (-2, -1, 0, 1, 2)
    if (di, dj) not in ((0, 0), (-1, 2), (1, -2))
]
AROUND = [(di, dj) for di in (-1, 0, 1) for dj in (-1, 0, 1) if (di, dj) != (0, 0)]


def first_kernel(
    owner_ref, block_ref, count_ref, tok_ref, ocean_ref, mask_ref, overlay_ref, proj_ref, grid_ref,
    msgs_ref, east_ref, south_ref, corner_ref, above_ref, below_ref, left_ref, right_ref, oc_ref, bias_ref,
    msg_s, east_s, corner_s, left_s, right_s, oc_s, table_s, send_sem, recv_sem,
):
    at = place()
    lo = lax.axis_index("lon")
    nlo = lax.axis_size("lon")
    wait_barrier = greet([at(*o) for o in SURFACE_PARTNERS])

    top, middle, last = split3(proj_ref[...])
    parts = jnp.concatenate([top, middle, last], axis=0).astype(BF16)
    state = ocean_ref[...].reshape(512, 256)
    surf = dot(parts, state, NT)
    surf = ((surf[0:8] + surf[8:16] + surf[16:24]) * mask_ref[...]).astype(BF16)
    row = iota((8, 128), 0)
    twice = []
    codes = jnp.full((8, 128), -1.0, F32)
    for k in range(3):
        block = overlay_ref[k]
        twice.append(dot(surf, jnp.concatenate([block, block], axis=0), NT))
        side = lax.rem(owner_ref[0, k] - lo + 1 + nlo, nlo)
        code = jnp.where(k < count_ref[0, 0], side * 8 + block_ref[0, k], -1).astype(F32)
        codes = jnp.where(row == 4 + k, code, codes)
    msg_s[0:8] = jnp.where(row < 4, twice[0], twice[1])
    msg_s[8:16] = jnp.where(row < 4, twice[2], codes)

    side = pack(tok_ref[4:16, 0:8, :].astype(F32), False)
    east_s[...] = side.reshape(48, 512).astype(BF16)
    side = pack(tok_ref[0:4, 0:8, :].astype(F32), False)
    corner_s[...] = side.reshape(16, 512).astype(BF16)
    west_cols = pack(ocean_ref[:, 0:8, :].astype(F32), False)
    east_cols = pack(ocean_ref[:, 24:32, :].astype(F32), True)
    left_s[...] = east_cols.reshape(64, 256).astype(BF16)
    right_s[...] = west_cols.reshape(64, 256).astype(BF16)
    oc_s[0] = west_cols[0:2].reshape(16, 256).astype(BF16)
    oc_s[1] = east_cols[0:2].reshape(16, 256).astype(BF16)
    oc_s[2] = west_cols[6:8].reshape(16, 256).astype(BF16)
    oc_s[3] = east_cols[6:8].reshape(16, 256).astype(BF16)

    copies = []

    def send(src, dst, offset):
        n = len(copies)
        copy = pltpu.make_async_remote_copy(
            src_ref=src, dst_ref=dst, send_sem=send_sem.at[n], recv_sem=recv_sem.at[n],
            device_id=at(*offset), device_id_type=MESH,
        )
        copies.append(copy)
        copy.start()

    wait_barrier()
    for below in range(2):
        for dj in (1, 2, -1, 0):
            if (below, dj) != (0, 0):
                send(msg_s, msgs_ref.at[below * 4 + dj + 1], (-below, -dj))
    send(east_s, east_ref, (0, -1))
    send(tok_ref.at[pl.ds(0, 4)], south_ref, (-1, 0))
    send(corner_s, corner_ref, (-1, -1))
    send(ocean_ref.at[pl.ds(0, 4)], below_ref, (-1, 0))
    send(ocean_ref.at[pl.ds(12, 4)], above_ref, (1, 0))
    send(left_s, left_ref, (0, 1))
    send(right_s, right_ref, (0, -1))
    send(oc_s.at[0], oc_ref.at[0], (-1, -1))
    send(oc_s.at[1], oc_ref.at[1], (-1, 1))
    send(oc_s.at[2], oc_ref.at[2], (1, -1))
    send(oc_s.at[3], oc_ref.at[3], (1, 1))
    msgs_ref[1] = msg_s[...]

    grid = jnp.concatenate([grid_ref[...], jnp.zeros((16, 31), F32)], axis=1)
    for ra in range(8):
        rolled = grid if ra == 0 else pltpu.roll(grid, 256 - 15 * ra, 1)
        table_s[:, ra, :] = rolled[:, 0:128]
    parts = [x.astype(BF16) for x in split3(table_s[...].reshape(128, 128))]
    entry = iota((128, 64), 0)
    lane = iota((128, 64), 1)
    for ca in range(8):
        chosen = (entry == (7 - lane // 8) * 15 + ca - lane % 8 + 7).astype(BF16)
        found = (dot(parts[0], chosen, NN) + dot(parts[1], chosen, NN)) + dot(parts[2], chosen, NN)
        bias_ref[:, ca, :] = found

    for copy in copies:
        copy.wait()


def vmem(n):
    return [pl.BlockSpec(memory_space=pltpu.VMEM)] * n


def smem(n):
    return [pl.BlockSpec(memory_space=pltpu.SMEM)] * n


def first(owners, blocks, counts, tok, ocean, mask_row, overlay, proj8, grid):
    shapes = [
        ((8, 16, 128), F32), ((48, 512), BF16), ((4, 24, 512), BF16), ((16, 512), BF16),
        ((4, 32, 256), BF16), ((4, 32, 256), BF16), ((64, 256), BF16), ((64, 256), BF16),
        ((4, 16, 256), BF16), ((128, 8, 64), F32),
    ]
    return pl.pallas_call(
        first_kernel,
        out_shape=[jax.ShapeDtypeStruct(*s) for s in shapes],
        in_specs=smem(3) + vmem(6),
        out_specs=vmem(len(shapes)),
        scratch_shapes=[
            pltpu.VMEM((16, 128), F32), pltpu.VMEM((48, 512), BF16), pltpu.VMEM((16, 512), BF16),
            pltpu.VMEM((64, 256), BF16), pltpu.VMEM((64, 256), BF16), pltpu.VMEM((4, 16, 256), BF16),
            pltpu.VMEM((16, 8, 128), F32),
            pltpu.SemaphoreType.DMA((18,)), pltpu.SemaphoreType.DMA((18,)),
        ],
        compiler_params=pltpu.CompilerParams(collective_id=0, has_side_effects=True),
        name="first",
    )(owners, blocks, counts, tok, ocean, mask_row, overlay, proj8, grid)


def layer_norm(x, gain, epsilon):
    average = jnp.mean(x, axis=-1, keepdims=True)
    centred = x - average
    spread = jnp.mean(centred * centred, axis=-1, keepdims=True)
    return centred * lax.rsqrt(spread + epsilon) * gain


def gather_surface(msgs_ref):
    row = iota((8, 128), 0)
    upper = row < 4
    right = iota((8, 128), 1) >= 64
    tiles = {}
    for below in range(2):
        for tile in range(2):
            sums = [jnp.zeros((8, 128), F32)] * 3
            for side in range(3):
                dj = tile - side + 1
                a = msgs_ref[below * 4 + dj + 1, 0:8, :]
                b = msgs_ref[below * 4 + dj + 1, 8:16, :]
                code_a = jnp.where(upper, b[4:5], b[5:6])
                code_b = jnp.where(upper, b[6:7], -1.0)
                for j in range(3):
                    target = jnp.where(right, side * 8.0 + 2 * j + 1, side * 8.0 + 2 * j)
                    sums[j] += jnp.where(code_a == target, a, 0.0) + jnp.where(code_b == target, b, 0.0)
            tiles[below, tile] = sums
    out = []
    for j in range(3):
        patch = iota((8, 128), 1) + 128 * j
        east = column_of(patch) < 4
        south = patch < 96
        here = jnp.where(east, tiles[0, 1][j], tiles[0, 0][j])
        under = jnp.where(east, tiles[1, 1][j], tiles[1, 0][j])
        out.append(jnp.where(south, under, here))
    return jnp.concatenate(out, axis=1)


def column_of(patch):
    p = patch.astype(F32)
    return p - 24.0 * jnp.floor((p + 0.5) * (1.0 / 24.0))


def atmosphere_kernel(
    tok_ref, east_ref, south_ref, corner_ref, msgs_ref, enc_ref, gain_ref, wqkv_ref, bqkv_ref, bias_ref, wo_ref, fp_ref,
    cyc_ref, flux_ref, pe_ref, pc_ref,
    mixed_s, norm_s, q_s, k_s, v_s, att_s, last_s,
):
    sst = gather_surface(msgs_ref)
    s_hi, s_lo = split2(sst)
    e_hi, e_lo = split2(enc_ref[...])
    left = jnp.concatenate([s_hi, s_lo, s_hi], axis=0).astype(BF16)
    right = jnp.concatenate([e_hi, e_hi, e_lo], axis=0).astype(BF16)
    mixed_s[...] = dot(left, right, TN).reshape(16, 24, 512)
    gain = gain_ref[...].reshape(1, 1, 512)
    for g in range(4):
        rows = slice(4 * g, 4 * g + 4)
        if g == 0:
            tokens = south_ref[...].astype(F32)
            side = unpack(corner_ref[...].astype(F32).reshape(2, 8, 512), False)
        else:
            tokens = tok_ref[rows].astype(F32)
            side = unpack(east_ref[16 * (g - 1) : 16 * g].astype(F32).reshape(2, 8, 512), False)
        head = jnp.where(low_half((4, 8, 512)), side, tokens[:, 0:8])
        tokens = jnp.concatenate([head, tokens[:, 8:24]], axis=1)
        mixed = (tokens + mixed_s[rows]).astype(BF16).astype(F32)
        mixed_s[rows] = mixed
        normed = layer_norm(mixed, gain, 1e-05)
        turned = [turn(normed[:, 8 * b : 8 * b + 8]) for b in range(3)]
        low = low_half((4, 8, 512))
        w_row, w_start = ((1, 4), (0, 0), (0, 4), (1, 0))[g]
        for b in range(3):
            norm_s[w_row * 3 + b, w_start : w_start + 4] = jnp.where(low, turned[b], turned[(b + 1) % 3])

    rows = norm_s[...].reshape(384, 512).astype(BF16)
    bq = bqkv_ref[...]
    q_s[...] = ((dot(rows, wqkv_ref[:, 0:512], NN) + bq[:, 0:512]) * 32 ** (-0.5)).astype(BF16)
    k_s[...] = (dot(rows, wqkv_ref[:, 512:1024], NN) + bq[:, 512:1024]).astype(BF16)
    v_s[...] = (dot(rows, wqkv_ref[:, 1024:1536], NN) + bq[:, 1024:1536]).astype(BF16)

    edge = lax.axis_index("lat") == lax.axis_size("lat") - 1
    a_row = (iota((512, 64), 0) % 64) >= 32
    b_row = iota((512, 64), 1) >= 32
    apart = jnp.where(a_row != b_row, -1e9, 0.0)
    last_s[...] = jnp.where(edge, apart, 0.0)
    own = (iota((8, 1, 256), 2) // 32) == iota((8, 1, 256), 0)

    def window(w, carry):
        lower = (w >= 3).astype(F32)
        at = pl.ds(pl.multiple_of(w * 64, 64), 64)
        for g in range(2):
            lanes = slice(256 * g, 256 * g + 256)
            queries = jnp.where(own, q_s[at, lanes][None], jnp.zeros((), BF16)).reshape(512, 256)
            scores = dot(queries, k_s[at, lanes], NT)
            scores = scores + bias_ref[64 * g : 64 * g + 64].reshape(512, 64) + lower * last_s[...]
            scores = scores - jnp.max(scores, axis=-1, keepdims=True)
            weights = jnp.exp(scores)
            weights = (weights / jnp.sum(weights, axis=-1, keepdims=True)).astype(BF16)
            found = dot(weights, v_s[at, lanes], NN).reshape(8, 64, 256)
            att_s[at, lanes] = jnp.sum(jnp.where(own, found, 0.0), axis=0).astype(BF16)
        return carry

    lax.fori_loop(0, 6, window, 0)

    norm_s[...] = dot(att_s[...], wo_ref[...], NN).astype(BF16).astype(F32).reshape(6, 8, 8, 512)
    for g in range(4):
        w_row, w_start = ((1, 4), (0, 0), (0, 4), (1, 0))[g]
        turned = [turn(norm_s[w_row * 3 + b, w_start : w_start + 4]) for b in range(3)]
        low = low_half((4, 8, 512))
        back = jnp.concatenate([jnp.where(low, turned[b - 1], turned[b]) for b in range(3)], axis=1)
        rows = slice(4 * g, 4 * g + 4)
        result = (mixed_s[rows] + back).astype(BF16)
        mixed_s[rows] = result.astype(F32)
        cyc_ref[rows] = result
        side = pack(result.astype(F32)[:, 0:8], False).reshape(16, 512).astype(BF16)
        if g == 0:
            pc_ref[...] = side
        else:
            pe_ref[16 * (g - 1) : 16 * g] = side
    flux_ref[...] = dot(fp_ref[...], mixed_s[...].reshape(384, 512).astype(BF16), NT).astype(BF16)


def atmosphere(tok, east, south, corner, msgs, enc8, gain, wqkv, bqkv, bias, wo, fp):
    shapes = [((16, 24, 512), BF16), ((16, 384), BF16), ((48, 512), BF16), ((16, 512), BF16)]
    return pl.pallas_call(
        atmosphere_kernel,
        out_shape=[jax.ShapeDtypeStruct(*s) for s in shapes],
        in_specs=vmem(12),
        out_specs=vmem(len(shapes)),
        scratch_shapes=[
            pltpu.VMEM((16, 24, 512), F32), pltpu.VMEM((6, 8, 8, 512), F32),
            pltpu.VMEM((384, 512), BF16), pltpu.VMEM((384, 512), BF16), pltpu.VMEM((384, 512), BF16),
            pltpu.VMEM((384, 512), BF16), pltpu.VMEM((512, 64), F32),
        ],
        name="atmosphere",
    )(tok, east, south, corner, msgs, enc8, gain, wqkv, bqkv, bias, wo, fp)


FLUX_TO = [(below, 0 - dj) for below in range(2) for dj in (-2, -1, 0, 1) if (below, dj) != (0, 0)]
FLUX_PARTNERS = FLUX_TO + [(-di, -dj) for di, dj in FLUX_TO if (-di, -dj) not in FLUX_TO]


def second_kernel(
    cyc_ref, flux_ref, pe_ref, pc_ref, ocean_ref, above_ref, below_ref, left_ref, right_ref, oc_ref, kernel_ref, cbias_ref,
    fluxes_ref, west_ref, north_ref, nw_ref, conv_ref,
    pad_s, send_sem, recv_sem,
):
    at = place()
    wait_barrier = greet([at(*o) for o in FLUX_PARTNERS])
    copies = []

    def send(src, dst, offset):
        n = len(copies)
        copy = pltpu.make_async_remote_copy(
            src_ref=src, dst_ref=dst, send_sem=send_sem.at[n], recv_sem=recv_sem.at[n],
            device_id=at(*offset), device_id_type=MESH,
        )
        copies.append(copy)
        copy.start()

    wait_barrier()
    for below in range(2):
        for dj in (-1, -2, 1, 0):
            if (below, dj) != (0, 0):
                send(flux_ref, fluxes_ref.at[below * 4 + dj + 2], (below, -dj))
    send(pe_ref, west_ref, (0, 1))
    send(cyc_ref.at[pl.ds(0, 4)], north_ref, (1, 0))
    send(pc_ref, nw_ref, (1, 1))
    fluxes_ref[2] = flux_ref[...]

    la = lax.axis_index("lat")
    has_above = (la > 0).astype(F32)
    has_below = (la < lax.axis_size("lat") - 1).astype(F32)

    def put(rows, cols, values):
        for h in range(2):
            pad_s[h, rows, cols, :] = values[:, :, 128 * h : 128 * h + 128]

    def wide(values, high):
        return unpack(values.astype(F32).reshape(values.shape[0] // 8, 8, 256), high)

    put(slice(3, 19), slice(8, 40), ocean_ref[...].astype(F32))
    put(slice(3, 19), slice(0, 8), wide(left_ref[...], True))
    put(slice(3, 19), slice(40, 48), wide(right_ref[...], False))
    put(slice(0, 3), slice(8, 40), above_ref[...].astype(F32)[1:4] * has_above)
    put(slice(19, 22), slice(8, 40), below_ref[...].astype(F32)[0:3] * has_below)
    put(slice(0, 3), slice(0, 8), wide(oc_ref[3], True)[1:4] * has_above)
    put(slice(0, 3), slice(40, 48), wide(oc_ref[2], False)[1:4] * has_above)
    put(slice(19, 22), slice(0, 8), wide(oc_ref[1], True)[0:3] * has_below)
    put(slice(19, 22), slice(40, 48), wide(oc_ref[0], False)[0:3] * has_below)

    def band(i, carry):
        start = i * 8
        for h in range(2):
            lanes = slice(128 * h, 128 * h + 128)
            first_term = jnp.broadcast_to(cbias_ref[:, lanes], (8, 128))
            for b in range(4):
                sums = [first_term] * 8
                for v in range(7):
                    col = 8 * b + v + 5
                    cells = [pad_s[h, start + r, col : col + 8, :] for r in range(14)]
                    for u in range(7):
                        tap = kernel_ref[u, v : v + 1, lanes]
                        for r in range(8):
                            sums[r] = sums[r] + tap * cells[r + u]
                for r in range(8):
                    conv_ref[start + r, 8 * b : 8 * b + 8, lanes] = sums[r]
        return carry

    lax.fori_loop(0, 2, band, 0)
    for copy in copies:
        copy.wait()


def second(cyc, flux, pe, pc, ocean, above, below, left, right, oc, kernel, cbias):
    shapes = [
        ((8, 16, 384), BF16), ((48, 512), BF16), ((4, 24, 512), BF16), ((16, 512), BF16), ((16, 32, 256), F32),
    ]
    return pl.pallas_call(
        second_kernel,
        out_shape=[jax.ShapeDtypeStruct(*s) for s in shapes],
        in_specs=vmem(12),
        out_specs=vmem(len(shapes)),
        scratch_shapes=[
            pltpu.VMEM((2, 22, 48, 128), F32),
            pltpu.SemaphoreType.DMA((10,)), pltpu.SemaphoreType.DMA((10,)),
        ],
        compiler_params=pltpu.CompilerParams(collective_id=1, has_side_effects=True),
        name="second",
    )(cyc, flux, pe, pc, ocean, above, below, left, right, oc, kernel, cbias)


def ocean_kernel(
    owner_ref, block_ref, count_ref, fluxes_ref, conv_ref, overlay_ref, fenc_ref, gain_ref, w1_ref, w2_ref, ocean_ref,
    mask_ref, scale_ref, cyc_ref, west_ref, north_ref, nw_ref,
    atm_ref, out_ref,
    pre_s, rate_s,
):
    lo = lax.axis_index("lon")
    nlo = lax.axis_size("lon")
    lane = iota((16, 128), 1)
    right = lane >= 64
    picked = [jnp.zeros((16, 128), F32)] * 3
    codes = []
    for k in range(3):
        side = lax.rem(owner_ref[0, k] - lo + 1 + nlo, nlo)
        codes.append(jnp.where(k < count_ref[0, 0], side * 8 + block_ref[0, k], -1))
    for j in range(3):
        patch = lane + 128 * j
        east = column_of(patch) < 4
        south = patch < 96
        at = slice(128 * j, 128 * j + 128)
        for side in range(3):
            here = jnp.where(east, fluxes_ref[side, :, at].astype(F32), fluxes_ref[side + 1, :, at].astype(F32))
            under = jnp.where(east, fluxes_ref[4 + side, :, at].astype(F32), fluxes_ref[5 + side, :, at].astype(F32))
            tile = jnp.where(south, under, here)
            target = jnp.where(right, side * 8 + 2 * j + 1, side * 8 + 2 * j)
            for k in range(3):
                picked[k] += jnp.where(target == codes[k], tile, 0.0)
    picked = [x + pltpu.roll(x, 64, 1) for x in picked]
    columns = jnp.concatenate([jnp.where(right, picked[1], picked[0]), picked[2][:, 0:64]], axis=1)
    forcing = dot(columns.astype(BF16), overlay_ref[...].reshape(192, 512), NN)
    f_hi, f_lo = split2(forcing)
    e_hi, e_lo = split2(fenc_ref[...])
    pre_s[...] = conv_ref[...].reshape(512, 256) + dot(
        jnp.concatenate([f_hi, f_lo, f_hi], axis=0).astype(BF16),
        jnp.concatenate([e_hi, e_hi, e_lo], axis=0).astype(BF16),
        TN,
    )
    mask = jnp.broadcast_to(mask_ref[...], (16, 512)).astype(BF16)
    parts = [jnp.broadcast_to(x, (16, 256)) for x in split3(scale_ref[...])]
    row = iota((16, 256), 0)
    scale = jnp.where(row == 0, parts[0], jnp.where(row == 1, parts[1], jnp.where(row == 2, parts[2], 0.0)))
    rate_s[...] = dot(mask, scale.astype(BF16), TN)

    def cells(i, carry):
        at = pl.ds(pl.multiple_of(i * 128, 128), 128)
        normed = layer_norm(pre_s[at], gain_ref[...], 1e-06).astype(BF16)
        update = jnp.zeros((128, 256), F32)
        for c in range(4):
            cols = slice(256 * c, 256 * c + 256)
            x = dot(normed, w1_ref[:, cols], NN)
            hidden = (0.5 * x * (1.0 + lax.erf(x * (0.5**0.5)))).astype(BF16)
            update = update + dot(hidden, w2_ref[cols], NN)
        rows = pl.ds(i * 4, 4)
        state = ocean_ref[rows].astype(F32).reshape(128, 256)
        out_ref[rows] = (state + rate_s[at] * update).astype(BF16).reshape(4, 32, 256)
        return carry

    lax.fori_loop(0, 4, cells, 0)

    low = low_half((4, 8, 512))
    for g in range(4):
        rows = slice(4 * g, 4 * g + 4)
        if g == 0:
            body = north_ref[...]
            side = nw_ref[...]
        else:
            body = cyc_ref[rows]
            side = west_ref[16 * (g - 1) : 16 * g]
        side = unpack(side.astype(F32).reshape(2, 8, 512), False)
        body = body.astype(F32)
        head = jnp.where(low, side, body[:, 0:8])
        atm_ref[rows] = jnp.concatenate([head, body[:, 8:24]], axis=1).astype(BF16)


def ocean_step(owners, blocks, counts, fluxes, conv, overlay, fenc, gain, w1, w2, ocean, mask_row, scale, cyc, west, north, nw):
    shapes = [((16, 24, 512), BF16), ((16, 32, 256), BF16)]
    return pl.pallas_call(
        ocean_kernel,
        out_shape=[jax.ShapeDtypeStruct(*s) for s in shapes],
        in_specs=smem(3) + vmem(14),
        out_specs=vmem(len(shapes)),
        scratch_shapes=[pltpu.VMEM((512, 256), F32), pltpu.VMEM((512, 256), F32)],
        name="ocean",
    )(owners, blocks, counts, fluxes, conv, overlay, fenc, gain, w1, w2, ocean, mask_row, scale, cyc, west, north, nw)


def local(
    atmos_patch_tokens,
    atmos_norm_gain,
    query_key_value_weight,
    query_key_value_bias,
    relative_bias_grid,
    attention_output_weight,
    flux_projector,
    surface_encoder,
    ocean_cell_state,
    land_sea_mask,
    depthwise_conv_kernel,
    depthwise_conv_bias,
    ocean_norm_gain,
    pointwise_expand,
    pointwise_contract,
    layer_update_scale,
    forcing_encoder,
    surface_projector,
    overlay_area_weight,
    owners,
    owner_tile_blocks,
    counts,
):
    owners = owners.reshape(1, 3)
    blocks = owner_tile_blocks.reshape(1, 3)
    overlay = overlay_area_weight.reshape(3, 64, 512)
    mask_row = land_sea_mask.reshape(1, 512).astype(F32)
    proj = surface_projector.T
    proj8 = jnp.concatenate([proj, proj], axis=0)
    enc8 = jnp.concatenate([surface_encoder, surface_encoder], axis=0)
    msgs, east, south, corner, above, below, left, right, oc, bias = first(
        owners, blocks, counts, atmos_patch_tokens, ocean_cell_state, mask_row, overlay, proj8, relative_bias_grid
    )
    cyc, flux, pe, pc = atmosphere(
        atmos_patch_tokens, east, south, corner, msgs, enc8, atmos_norm_gain.reshape(1, 512), query_key_value_weight,
        query_key_value_bias.reshape(1, 1536), bias, attention_output_weight, flux_projector.T,
    )
    fluxes, west, north, nw, conv = second(
        cyc, flux, pe, pc, ocean_cell_state, above, below, left, right, oc, depthwise_conv_kernel,
        depthwise_conv_bias.reshape(1, 256),
    )
    atm_out, ocean_out = ocean_step(
        owners, blocks, counts, fluxes, conv, overlay, forcing_encoder, ocean_norm_gain.reshape(1, 256), pointwise_expand,
        pointwise_contract, ocean_cell_state, mask_row, layer_update_scale.reshape(1, 256), cyc, west, north, nw,
    )
    return atm_out, ocean_out


def solution(mesh):
    rep = P()
    placed = (
        P("lat", "lon", None), rep, rep, rep, rep, rep, rep, rep, P("lat", "lon", None), P("lat", "lon"),
        rep, rep, rep, rep, rep, rep, rep, rep, P("lat", "lon", None, None, None),
        P("lat", "lon", None), P("lat", "lon", None), P("lat", "lon"),
    )
    return jax.shard_map(
        local,
        mesh=mesh,
        in_specs=placed,
        out_specs=(P("lat", "lon", None), P("lat", "lon", None)),
        check_vma=False,
    )
```

time: 138 us -> 77.4 us (0.56)
  the two profiles are of different devices: /device:TPU:8 before, /device:TPU:1 now
where the time goes in v1:
time: 77.4 us; the launch traced here: 76.5 us
  Pallas kernels  69.8 us (90%)
  other arithmetic  3.45 us (4%)
  local copies, waits for them, and re-layouts  1.94 us (3%)
  between operations  1.3 us (2%)
    pallas_call x1, Pallas kernels, first(): pl.pallas_call(first_kernel, out_shape=[jax.ShapeDtypeStruct(*s) for s in...  35 us
    pallas_call x1, Pallas kernels, second(): pl.pallas_call(second_kernel, out_shape=[jax.ShapeDtypeStruct(*s) for s i...  18.1 us
    pallas_call x1, Pallas kernels, atmosphere(): pl.pallas_call(atmosphere_kernel, out_shape=[jax.ShapeDtypeStruct(*s) for...  11.3 us
    pallas_call x1, Pallas kernels, ocean_step(): pl.pallas_call(ocean_kernel, out_shape=[jax.ShapeDtypeStruct(*s) for s in...  5.46 us

profile of v1, /device:TPU:1, one launch (start us, length us, event | category | flops | bytes accessed | tf_op | source)
XLA Modules:
  0.0 76.5 jit_solution(10066229918394422864)
XLA Ops:
  1.3 1.3 %reshape.46.bqkv_ref = f32[1,1536]{1,0:T(1,128)} reshape(f32[1536]{0:T(1024)} %param.25) | data formatting | bytes 12288 | tf_op jit(solution)/shard_map/reshape | solution.py:553
  2.6 0.7 convert_element_type.5
  3.3 0.7 convert_element_type.6.mask_ref
  3.9 1.4 %pad_maximum_fusion.1.proj_ref = f32[8,256]{1,0:T(8,128)} fusion(f32[4,256]{1,0:T(4,128)} %bitcast.12), kind=kLoop, calls=%fused_computation.1 | loop fusion | flops 2048 | bytes 12288 | tf_op jit(solution)/shard_map/concatenate | solution.py:546
  5.3 1.4 %pad_maximum_fusion.enc_ref = f32[8,512]{1,0:T(8,128)} fusion(f32[4,512]{1,0:T(4,128)} %param.29), kind=kLoop, calls=%fused_computation | loop fusion | flops 4096 | bytes 24576 | tf_op jit(solution)/shard_map/concatenate | solution.py:547
  6.7 35.0 %first.1 = (f32[8,16,128]{2,1,0:T(8,128)}, bf16[48,512]{1,0:T(8,128)(2,1)}, bf16[4,24,512]{2,1,0:T(8,128)(2,1)}, bf16[16,512]{1,0:T(8,128)(2,1)}, bf16[4,32,256]...) custom-call(s32[1,3]{1,0:T(1,128)} %bitcast.14, ...), custom_call_target="tpu_custom_call" | custom-call | tf_op jit(solution)/shard_map/first/pallas_call | solution.py:185
  41.7 11.3 %atmosphere.1 = (bf16[16,24,512]{2,1,0:T(8,128)(2,1)}, bf16[16,384]{1,0:T(8,128)(2,1)}, bf16[48,512]{1,0:T(8,128)(2,1)}, bf16[16,512]{1,0:T(8,128)(2,1)}) custom-call(bf16[16,24,512]{2,1,0:T(8,128)(2,1)} %tok_ref.3, bf16[48,512]{1,0:T(8,128)(2,1)} %get-tuple-element.21.east_ref, bf16[4,24,512]{2,1,0:T(8,128)(2,1)} %get-tuple-element.22.south_ref, ...), custom_call_target="tpu_custom_call" | custom-call | tf_op jit(solution)/shard_map/atmosphere/pallas_call | solution.py:323
  53.0 18.1 %second.1 = (bf16[8,16,384]{2,1,0:T(8,128)(2,1)}, bf16[48,512]{1,0:T(8,128)(2,1)}, bf16[4,24,512]{2,1,0:T(8,128)(2,1)}, bf16[16,512]{1,0:T(8,128)(2,1)}, f32[16,32,256]{2,1,0:T(8,128)}) custom-call(bf16[16,24,512]{2,1,0:T(8,128)(2,1)} %get-tuple-element.26.cyc_ref, bf16[16,384]{1,0:T(8,128)(2,1)} %get-tuple-element.27.flux_ref, ...), custom_call_target="tpu_custom_call" | custom-call | tf_op jit(solution)/shard_map/second/pallas_call | solution.py:417
  71.0 5.5 %ocean.1 = (bf16[16,24,512]{2,1,0:T(8,128)(2,1)}, bf16[16,32,256]{2,1,0:T(8,128)(2,1)}) custom-call(s32[1,3]{1,0:T(1,128)} %bitcast.15, s32[1,3]{1,0:T(1,128)} %bitcast.17, s32[1,1]{1,0:T(1,128)S(6)} %copy.24.count_ref, bf16[8,16,384]{2,1,0:T(8,128)(2,1)} %get-tuple-element.35.fluxes_ref, f32[16,32,256]{2,1,0:T(8,128)} %get-tuple-element.36.conv_ref, ...), custom_call_target="tpu_custom_call" | custom-call | tf_op jit(solution)/shard_map/ocean/pallas_call | solution.py:507

commit v2 on v1

v2 whole, which is shorter than its diff:
```python
import functools

import jax
import jax.numpy as jnp
from jax import lax
from jax.experimental import pallas as pl
from jax.experimental.pallas import tpu as pltpu
from jax.sharding import PartitionSpec as P

F32 = jnp.float32
BF16 = jnp.bfloat16
MESH = pl.DeviceIdType.MESH
HEADS = 16
HALF = 8
WIN = 8
NT = (((1,), (1,)), ((), ()))
TN = (((0,), (0,)), ((), ()))
NN = (((1,), (0,)), ((), ()))


def dot(a, b, dims):
    return lax.dot_general(a, b, dims, preferred_element_type=F32)


def iota(shape, dim):
    return lax.broadcasted_iota(jnp.int32, shape, dim)


def low_half(shape):
    return iota(shape, len(shape) - 2) % 8 < 4


def turn(x):
    return pltpu.roll(x, 4, x.ndim - 2)


def pack(x, high):
    n, _, lanes = x.shape
    x = x.reshape(n // 2, 2, 8, lanes)
    even, odd = x[:, 0], x[:, 1]
    if high:
        even = turn(even)
    else:
        odd = turn(odd)
    return jnp.where(low_half(even.shape), even, odd)


def unpack(x, high):
    n, _, lanes = x.shape
    other = turn(x)
    pair = (other, x) if high else (x, other)
    return jnp.stack(pair, axis=1).reshape(2 * n, 8, lanes)


def split2(x):
    top = x.astype(BF16).astype(F32)
    return top, x - top


def split3(x):
    top, rest = split2(x)
    middle, last = split2(rest)
    return top, middle, last


def greet(partners):
    barrier = pltpu.get_barrier_semaphore()
    for device in partners:
        pl.semaphore_signal(barrier, inc=1, device_id=device, device_id_type=MESH)
    return lambda: pl.semaphore_wait(barrier, len(partners))


def place():
    la, lo = lax.axis_index("lat"), lax.axis_index("lon")
    nla, nlo = lax.axis_size("lat"), lax.axis_size("lon")
    return lambda di, dj: (lax.rem(la + di + nla, nla), lax.rem(lo + dj + nlo, nlo))


def vmem(n):
    return [pl.BlockSpec(memory_space=pltpu.VMEM)] * n


def smem(n):
    return [pl.BlockSpec(memory_space=pltpu.SMEM)] * n


def anywhere(n):
    return [pl.BlockSpec(memory_space=pl.ANY)] * n


def layer_norm(x, gain, epsilon):
    average = jnp.mean(x, axis=-1, keepdims=True)
    centred = x - average
    spread = jnp.mean(centred * centred, axis=-1, keepdims=True)
    return centred * lax.rsqrt(spread + epsilon) * gain


def column_of(patch):
    p = patch.astype(F32)
    return p - 24.0 * jnp.floor((p + 0.5) * (1.0 / 24.0))


def mask_row(mask):
    wide = jnp.concatenate([mask.astype(F32), jnp.zeros((16, 96), F32)], axis=1)
    moved = [wide if q == 0 else pltpu.roll(wide, 32 * q, 1) for q in range(4)]
    parts = [sum(moved[q][4 * j + q : 4 * j + q + 1] for q in range(4)) for j in range(4)]
    return jnp.concatenate(parts, axis=1)


PARTNERS = [(0, 1), (0, -1), (0, 2), (0, -2), (1, 0), (-1, 0)]
COPIES = 32


def surface_message(owner_ref, block_ref, count_ref, ocean_ref, mask_ref, overlay_ref, proj_s, msg_s):
    lo = lax.axis_index("lon")
    nlo = lax.axis_size("lon")
    parts = jnp.concatenate(split3(proj_s[...]), axis=0).astype(BF16)
    surf = dot(parts, ocean_ref[...].reshape(512, 256), NT)
    surf = ((surf[0:8] + surf[8:16] + surf[16:24]) * mask_row(mask_ref[...])).astype(BF16)
    row = iota((8, 128), 0)
    twice = []
    codes = jnp.full((8, 128), -1.0, F32)
    for k in range(3):
        block = overlay_ref[k]
        twice.append(dot(surf, jnp.concatenate([block, block], axis=0), NT))
        side = lax.rem(owner_ref[0, k] - lo + 1 + nlo, nlo)
        code = jnp.where(k < count_ref[0, 0], side * 8 + block_ref[0, k], -1).astype(F32)
        codes = jnp.where(row == 4 + k, code, codes)
    msg_s[0:8] = jnp.where(row < 4, twice[0], twice[1])
    msg_s[8:16] = jnp.where(row < 4, twice[2], codes)


def gather_surface(msgs_ref):
    upper = iota((8, 128), 0) < 4
    right = iota((8, 128), 1) >= 64
    tiles = []
    for tile in range(2):
        sums = [jnp.zeros((8, 128), F32)] * 3
        for side in range(3):
            slot = tile - side + 2
            a = msgs_ref[slot, 0:8, :]
            b = msgs_ref[slot, 8:16, :]
            code_a = jnp.where(upper, b[4:5], b[5:6])
            code_b = jnp.where(upper, b[6:7], -1.0)
            for j in range(3):
                target = jnp.where(right, side * 8.0 + 2 * j + 1, side * 8.0 + 2 * j)
                sums[j] += jnp.where(code_a == target, a, 0.0) + jnp.where(code_b == target, b, 0.0)
        tiles.append(sums)
    return [
        jnp.where(column_of(iota((8, 128), 1) + 128 * j) < 4, tiles[1][j], tiles[0][j]) for j in range(3)
    ]


def bias_table(grid_ref, table_s, bias_s):
    grid = jnp.concatenate([grid_ref[...], jnp.zeros((16, 31), F32)], axis=1)
    for ra in range(8):
        rolled = grid if ra == 0 else pltpu.roll(grid, 256 - 15 * ra, 1)
        table_s[:, ra, :] = rolled[:, 0:128]
    parts = [x.astype(BF16) for x in split3(table_s[...].reshape(128, 128))]
    entry = iota((128, 64), 0)
    lane = iota((128, 64), 1)
    for ca in range(8):
        chosen = (entry == (7 - lane // 8) * 15 + ca - lane % 8 + 7).astype(BF16)
        found = (dot(parts[0], chosen, NN) + dot(parts[1], chosen, NN)) + dot(parts[2], chosen, NN)
        bias_s[:, ca, :] = found


def add_surface(sst, enc_s):
    s_hi, s_lo = split2(sst)
    e_hi, e_lo = split2(enc_s[...])
    left = jnp.concatenate([s_hi, s_lo, s_hi], axis=0).astype(BF16)
    right = jnp.concatenate([e_hi, e_hi, e_lo], axis=0).astype(BF16)
    return dot(left, right, TN)


def normalise(g, tokens, side, gain, mixed_s, norm_s):
    low = low_half((4, 8, 512))
    rows = slice(4 * g, 4 * g + 4)
    tokens = tokens.astype(F32)
    side = unpack(side.astype(F32).reshape(2, 8, 512), False)
    head = jnp.where(low, side, tokens[:, 0:8])
    tokens = jnp.concatenate([head, tokens[:, 8:24]], axis=1)
    mixed = (tokens + mixed_s[rows]).astype(BF16).astype(F32)
    mixed_s[rows] = mixed
    normed = layer_norm(mixed, gain, 1e-05)
    turned = [turn(normed[:, 8 * b : 8 * b + 8]) for b in range(3)]
    w_row, w_start = WINDOW_OF[g]
    for b in range(3):
        norm_s[w_row * 3 + b, w_start : w_start + 4] = jnp.where(low, turned[b], turned[(b + 1) % 3])


WINDOW_OF = ((1, 4), (0, 0), (0, 4), (1, 0))


def attend(w_row, norm_s, wqkv_s, bqkv_ref, wo_s, bias_s, last_s, q_s, k_s, v_s, att_s):
    rows = norm_s[3 * w_row : 3 * w_row + 3].reshape(192, 512).astype(BF16)
    for part, ref in enumerate((q_s, k_s, v_s)):
        cols = slice(512 * part, 512 * part + 512)
        value = dot(rows, wqkv_s[:, cols], NN) + bqkv_ref[cols].reshape(1, 512)
        if part == 0:
            value = value * 32 ** (-0.5)
        ref[...] = value.astype(BF16)
    own = (iota((8, 1, 256), 2) // 32) == iota((8, 1, 256), 0)

    def window(w, carry):
        at = pl.ds(pl.multiple_of(w * 64, 64), 64)
        for g in range(2):
            lanes = slice(256 * g, 256 * g + 256)
            queries = jnp.where(own, q_s[at, lanes][None], jnp.zeros((), BF16)).reshape(512, 256)
            scores = dot(queries, k_s[at, lanes], NT)
            scores = scores + bias_s[64 * g : 64 * g + 64].reshape(512, 64)
            if w_row == 1:
                scores = scores + last_s[...]
            scores = scores - jnp.max(scores, axis=-1, keepdims=True)
            weights = jnp.exp(scores)
            weights = (weights / jnp.sum(weights, axis=-1, keepdims=True)).astype(BF16)
            found = dot(weights, v_s[at, lanes], NN).reshape(8, 64, 256)
            att_s[at, lanes] = jnp.sum(jnp.where(own, found, 0.0), axis=0).astype(BF16)
        return carry

    lax.fori_loop(0, 3, window, 0)
    projected = dot(att_s[...], wo_s[...], NN).astype(BF16).astype(F32)
    norm_s[3 * w_row : 3 * w_row + 3] = projected.reshape(3, 8, 8, 512)


def finish(g, norm_s, mixed_s, cyc_ref, side_ref):
    w_row, w_start = WINDOW_OF[g]
    turned = [turn(norm_s[w_row * 3 + b, w_start : w_start + 4]) for b in range(3)]
    low = low_half((4, 8, 512))
    back = jnp.concatenate([jnp.where(low, turned[b - 1], turned[b]) for b in range(3)], axis=1)
    rows = slice(4 * g, 4 * g + 4)
    result = (mixed_s[rows] + back).astype(BF16)
    mixed_s[rows] = result.astype(F32)
    cyc_ref[rows] = result
    side_ref[...] = pack(result.astype(F32)[:, 0:8], False).reshape(16, 512).astype(BF16)


def convolve(pad_s, kernel_ref, cbias_ref, conv_ref):
    def band(i, carry):
        start = i * 8
        for h in range(2):
            lanes = slice(128 * h, 128 * h + 128)
            first_term = jnp.broadcast_to(cbias_ref[:, lanes], (8, 128))
            for b in range(4):
                sums = [first_term] * 8
                for v in range(7):
                    col = 8 * b + v + 5
                    cells = [pad_s[h, start + r, col : col + 8, :] for r in range(14)]
                    for u in range(7):
                        tap = kernel_ref[u, v : v + 1, lanes]
                        for r in range(8):
                            sums[r] = sums[r] + tap * cells[r + u]
                for r in range(8):
                    conv_ref[start + r, 8 * b : 8 * b + 8, lanes] = sums[r]
        return carry

    lax.fori_loop(0, 2, band, 0)


def step_kernel(
    owner_ref, block_ref, count_ref, tok_ref, ocean_ref, mask_ref, overlay_ref, proj_ref, grid_ref, enc_ref, gain_ref, bqkv_ref,
    fp_ref, kernel_ref, cbias_ref, wqkv_ref, wo_ref,
    cyc_ref, fluxes_ref, west_ref, north_ref, nw_ref, conv_ref,
    wqkv_s, wo_s, proj_s, enc_s, msg_s, msgs_s, side_s, east_s, south_s, corner_s, sst_s, under_s, table_s, bias_s, last_s,
    mixed_s, norm_s, q_s, k_s, v_s, att_s, above_s, below_s, leave_s, cols_s, pad_s, pe_s, flux_s,
    load_sem, send_sem, recv_sem,
):
    at = place()
    la = lax.axis_index("lat")
    nla = lax.axis_size("lat")
    wait_barrier = greet([at(*o) for o in PARTNERS])
    loads = [
        pltpu.make_async_copy(wqkv_ref, wqkv_s, load_sem.at[0]),
        pltpu.make_async_copy(wo_ref, wo_s, load_sem.at[1]),
    ]
    for load in loads:
        load.start()
    copies = []

    def send(src, dst, offset):
        n = len(copies)
        copy = pltpu.make_async_remote_copy(
            src_ref=src, dst_ref=dst, send_sem=send_sem.at[n], recv_sem=recv_sem.at[n],
            device_id=at(*offset), device_id_type=MESH,
        )
        copies.append(copy)
        copy.start()
        return copy

    for half in range(2):
        proj_s[4 * half : 4 * half + 4] = proj_ref[...]
        enc_s[4 * half : 4 * half + 4] = enc_ref[...]
    surface_message(owner_ref, block_ref, count_ref, ocean_ref, mask_ref, overlay_ref, proj_s, msg_s)
    side_s[...] = pack(tok_ref[:, 0:8, :].astype(F32), False).reshape(64, 512).astype(BF16)

    wait_barrier()
    messages = [send(msg_s, msgs_s.at[dj + 1], (0, -dj)) for dj in (2, 1, -1)]
    msgs_s[1] = msg_s[...]
    east = send(side_s, east_s, (0, -1))

    bias_table(grid_ref, table_s, bias_s)
    edge = la == nla - 1
    a_row = (iota((512, 64), 0) % 64) >= 32
    b_row = iota((512, 64), 1) >= 32
    last_s[...] = jnp.where(edge, jnp.where(a_row != b_row, -1e9, 0.0), 0.0)

    for copy in messages:
        copy.wait_recv()
    sst = gather_surface(msgs_s)
    sst_s[...] = sst[0]
    under = send(sst_s, under_s, (-1, 0))
    south = send(tok_ref.at[pl.ds(0, 4)], south_s, (-1, 0))
    below = send(ocean_ref.at[pl.ds(0, 3)], below_s, (-1, 0))
    above = send(ocean_ref.at[pl.ds(13, 3)], above_s, (1, 0))
    mixed_s[...] = add_surface(jnp.concatenate(sst, axis=1), enc_s).reshape(16, 24, 512)
    gain = gain_ref[...].reshape(1, 1, 512)
    east.wait_recv()
    corner = send(east_s.at[pl.ds(0, 16)], corner_s, (-1, 0))
    for g in (1, 2, 3):
        normalise(g, tok_ref[4 * g : 4 * g + 4], east_s[16 * g : 16 * g + 16], gain, mixed_s, norm_s)
    for load in loads:
        load.wait()
    attend(0, norm_s, wqkv_s, bqkv_ref, wo_s, bias_s, last_s, q_s, k_s, v_s, att_s)
    for g in (1, 2):
        finish(g, norm_s, mixed_s, cyc_ref, pe_s.at[pl.ds(16 * g, 16)])
    send(pe_s.at[pl.ds(16, 32)], west_ref.at[pl.ds(16, 32)], (0, 1))

    def put(rows, cols, values):
        for h in range(2):
            pad_s[h, rows, cols, :] = values[:, :, 128 * h : 128 * h + 128]

    below.wait_recv()
    above.wait_recv()
    put(slice(3, 19), slice(8, 40), ocean_ref[...].astype(F32))
    put(slice(0, 3), slice(8, 40), above_s[...].astype(F32) * (la > 0).astype(F32))
    put(slice(19, 22), slice(8, 40), below_s[...].astype(F32) * (la < nla - 1).astype(F32))
    for h in range(2):
        lanes = slice(128 * h, 128 * h + 128)
        leave_s[0, :, lanes] = pack(pad_s[h, :, 32:40, :], True).reshape(88, 128).astype(BF16)
        leave_s[1, :, lanes] = pack(pad_s[h, :, 8:16, :], False).reshape(88, 128).astype(BF16)
    sides = [send(leave_s.at[0], cols_s.at[0], (0, 1)), send(leave_s.at[1], cols_s.at[1], (0, -1))]

    for copy in (under, south, corner):
        copy.wait_recv()
    mixed_s[0:4] = add_surface(under_s[...], enc_s)[0:96].reshape(4, 24, 512)
    normalise(0, south_s[...], corner_s[...], gain, mixed_s, norm_s)
    attend(1, norm_s, wqkv_s, bqkv_ref, wo_s, bias_s, last_s, q_s, k_s, v_s, att_s)
    for g in (3, 0):
        finish(g, norm_s, mixed_s, cyc_ref, pe_s.at[pl.ds(16 * g, 16)])
    flux_s[...] = dot(fp_ref[...], mixed_s[...].reshape(384, 512).astype(BF16), NT).astype(BF16)
    for down in (1, 0):
        for dj in (1, -2, -1, 0):
            if (down, dj) != (0, 0):
                send(flux_s, fluxes_ref.at[down * 4 + dj + 2], (down, -dj))
    send(cyc_ref.at[pl.ds(0, 4)], north_ref, (1, 0))
    send(pe_s.at[pl.ds(48, 16)], west_ref.at[pl.ds(48, 16)], (0, 1))
    send(pe_s.at[pl.ds(0, 16)], nw_ref, (1, 1))
    fluxes_ref[2] = flux_s[...]

    for copy in sides:
        copy.wait_recv()
    for n, high in ((0, True), (1, False)):
        values = unpack(cols_s[n].astype(F32).reshape(11, 8, 256), high)
        put(slice(0, 22), slice(40 * n, 40 * n + 8), values)
    convolve(pad_s, kernel_ref, cbias_ref, conv_ref)

    early = [*messages, east, under, south, below, above, corner, *sides]
    for copy in copies:
        copy.wait_send()
        if not any(copy is other for other in early):
            copy.wait_recv()


def step(owners, blocks, counts, tok, ocean, mask, overlay, proj, grid, enc, gain, bqkv, fp, kernel, cbias, wqkv, wo):
    shapes = [
        ((16, 24, 512), BF16), ((8, 16, 384), BF16), ((64, 512), BF16), ((4, 24, 512), BF16), ((16, 512), BF16),
        ((16, 32, 256), F32),
    ]
    return pl.pallas_call(
        step_kernel,
        out_shape=[jax.ShapeDtypeStruct(*s) for s in shapes],
        in_specs=smem(3) + vmem(12) + anywhere(2),
        out_specs=vmem(len(shapes)),
        scratch_shapes=[
            pltpu.VMEM((512, 1536), BF16), pltpu.VMEM((512, 512), BF16), pltpu.VMEM((8, 256), F32), pltpu.VMEM((8, 512), F32),
            pltpu.VMEM((16, 128), F32), pltpu.VMEM((4, 16, 128), F32), pltpu.VMEM((64, 512), BF16), pltpu.VMEM((64, 512), BF16),
            pltpu.VMEM((4, 24, 512), BF16), pltpu.VMEM((16, 512), BF16), pltpu.VMEM((8, 128), F32), pltpu.VMEM((8, 128), F32),
            pltpu.VMEM((16, 8, 128), F32), pltpu.VMEM((128, 8, 64), F32), pltpu.VMEM((512, 64), F32),
            pltpu.VMEM((16, 24, 512), F32), pltpu.VMEM((6, 8, 8, 512), F32),
            pltpu.VMEM((192, 512), BF16), pltpu.VMEM((192, 512), BF16), pltpu.VMEM((192, 512), BF16), pltpu.VMEM((192, 512), BF16),
            pltpu.VMEM((3, 32, 256), BF16), pltpu.VMEM((3, 32, 256), BF16), pltpu.VMEM((2, 88, 256), BF16),
            pltpu.VMEM((2, 88, 256), BF16), pltpu.VMEM((2, 22, 48, 128), F32), pltpu.VMEM((64, 512), BF16),
            pltpu.VMEM((16, 384), BF16),
            pltpu.SemaphoreType.DMA((2,)), pltpu.SemaphoreType.DMA((COPIES,)), pltpu.SemaphoreType.DMA((COPIES,)),
        ],
        compiler_params=pltpu.CompilerParams(collective_id=0, has_side_effects=True),
        name="step",
    )(owners, blocks, counts, tok, ocean, mask, overlay, proj, grid, enc, gain, bqkv, fp, kernel, cbias, wqkv, wo)


def ocean_kernel(
    owner_ref, block_ref, count_ref, fluxes_ref, conv_ref, overlay_ref, fenc_ref, gain_ref, w1_ref, w2_ref, ocean_ref,
    mask_ref, scale_ref, cyc_ref, west_ref, north_ref, nw_ref,
    atm_ref, out_ref,
    pre_s, rate_s,
):
    lo = lax.axis_index("lon")
    nlo = lax.axis_size("lon")
    lane = iota((16, 128), 1)
    right = lane >= 64
    picked = [jnp.zeros((16, 128), F32)] * 3
    codes = []
    for k in range(3):
        side = lax.rem(owner_ref[0, k] - lo + 1 + nlo, nlo)
        codes.append(jnp.where(k < count_ref[0, 0], side * 8 + block_ref[0, k], -1))
    for j in range(3):
        patch = lane + 128 * j
        east = column_of(patch) < 4
        south = patch < 96
        at = slice(128 * j, 128 * j + 128)
        for side in range(3):
            here = jnp.where(east, fluxes_ref[side, :, at].astype(F32), fluxes_ref[side + 1, :, at].astype(F32))
            under = jnp.where(east, fluxes_ref[4 + side, :, at].astype(F32), fluxes_ref[5 + side, :, at].astype(F32))
            tile = jnp.where(south, under, here)
            target = jnp.where(right, side * 8 + 2 * j + 1, side * 8 + 2 * j)
            for k in range(3):
                picked[k] += jnp.where(target == codes[k], tile, 0.0)
    picked = [x + pltpu.roll(x, 64, 1) for x in picked]
    columns = jnp.concatenate([jnp.where(right, picked[1], picked[0]), picked[2][:, 0:64]], axis=1)
    forcing = dot(columns.astype(BF16), overlay_ref[...].reshape(192, 512), NN)
    f_hi, f_lo = split2(forcing)
    e_hi, e_lo = split2(fenc_ref[...])
    pre_s[...] = conv_ref[...].reshape(512, 256) + dot(
        jnp.concatenate([f_hi, f_lo, f_hi], axis=0).astype(BF16),
        jnp.concatenate([e_hi, e_hi, e_lo], axis=0).astype(BF16),
        TN,
    )
    mask = jnp.broadcast_to(mask_row(mask_ref[...]), (16, 512)).astype(BF16)
    parts = [jnp.broadcast_to(x, (16, 256)) for x in split3(scale_ref[...])]
    row = iota((16, 256), 0)
    scale = jnp.where(row == 0, parts[0], jnp.where(row == 1, parts[1], jnp.where(row == 2, parts[2], 0.0)))
    rate_s[...] = dot(mask, scale.astype(BF16), TN)

    def cells(i, carry):
        at = pl.ds(pl.multiple_of(i * 128, 128), 128)
        normed = layer_norm(pre_s[at], gain_ref[...], 1e-06).astype(BF16)
        update = jnp.zeros((128, 256), F32)
        for c in range(4):
            cols = slice(256 * c, 256 * c + 256)
            x = dot(normed, w1_ref[:, cols], NN)
            hidden = (0.5 * x * (1.0 + lax.erf(x * (0.5**0.5)))).astype(BF16)
            update = update + dot(hidden, w2_ref[cols], NN)
        rows = pl.ds(i * 4, 4)
        state = ocean_ref[rows].astype(F32).reshape(128, 256)
        out_ref[rows] = (state + rate_s[at] * update).astype(BF16).reshape(4, 32, 256)
        return carry

    lax.fori_loop(0, 4, cells, 0)

    low = low_half((4, 8, 512))
    for g in range(4):
        rows = slice(4 * g, 4 * g + 4)
        if g == 0:
            body = north_ref[...]
            side = nw_ref[...]
        else:
            body = cyc_ref[rows]
            side = west_ref[16 * g : 16 * g + 16]
        side = unpack(side.astype(F32).reshape(2, 8, 512), False)
        body = body.astype(F32)
        head = jnp.where(low, side, body[:, 0:8])
        atm_ref[rows] = jnp.concatenate([head, body[:, 8:24]], axis=1).astype(BF16)


def ocean_step(owners, blocks, counts, fluxes, conv, overlay, fenc, gain, w1, w2, ocean, mask, scale, cyc, west, north, nw):
    shapes = [((16, 24, 512), BF16), ((16, 32, 256), BF16)]
    return pl.pallas_call(
        ocean_kernel,
        out_shape=[jax.ShapeDtypeStruct(*s) for s in shapes],
        in_specs=smem(3) + vmem(14),
        out_specs=vmem(len(shapes)),
        scratch_shapes=[pltpu.VMEM((512, 256), F32), pltpu.VMEM((512, 256), F32)],
        name="ocean",
    )(owners, blocks, counts, fluxes, conv, overlay, fenc, gain, w1, w2, ocean, mask, scale, cyc, west, north, nw)


def local(
    atmos_patch_tokens,
    atmos_norm_gain,
    query_key_value_weight,
    query_key_value_bias,
    relative_bias_grid,
    attention_output_weight,
    flux_projector,
    surface_encoder,
    ocean_cell_state,
    land_sea_mask,
    depthwise_conv_kernel,
    depthwise_conv_bias,
    ocean_norm_gain,
    pointwise_expand,
    pointwise_contract,
    layer_update_scale,
    forcing_encoder,
    surface_projector,
    overlay_area_weight,
    owners,
    owner_tile_blocks,
    counts,
):
    owners = owners.reshape(1, 3)
    blocks = owner_tile_blocks.reshape(1, 3)
    overlay = overlay_area_weight.reshape(3, 64, 512)
    cyc, fluxes, west, north, nw, conv = step(
        owners, blocks, counts, atmos_patch_tokens, ocean_cell_state, land_sea_mask, overlay, surface_projector.T,
        relative_bias_grid, surface_encoder, atmos_norm_gain.reshape(1, 512), query_key_value_bias, flux_projector.T,
        depthwise_conv_kernel, depthwise_conv_bias.reshape(1, 256), query_key_value_weight, attention_output_weight,
    )
    atm_out, ocean_out = ocean_step(
        owners, blocks, counts, fluxes, conv, overlay, forcing_encoder, ocean_norm_gain.reshape(1, 256), pointwise_expand,
        pointwise_contract, ocean_cell_state, land_sea_mask, layer_update_scale.reshape(1, 256), cyc, west, north, nw,
    )
    return atm_out, ocean_out


def solution(mesh):
    rep = P()
    placed = (
        P("lat", "lon", None), rep, rep, rep, rep, rep, rep, rep, P("lat", "lon", None), P("lat", "lon"),
        rep, rep, rep, rep, rep, rep, rep, rep, P("lat", "lon", None, None, None),
        P("lat", "lon", None), P("lat", "lon", None), P("lat", "lon"),
    )
    return jax.shard_map(
        local,
        mesh=mesh,
        in_specs=placed,
        out_specs=(P("lat", "lon", None), P("lat", "lon", None)),
        check_vma=False,
    )
```

time: 77.4 us -> 53.1 us (0.69)
  the two profiles are of different devices: /device:TPU:1 before, /device:TPU:8 now
where the time goes in v2:
time: 53.1 us; the launch traced here: 52.9 us
  Pallas kernels  51.6 us (97%)
  between operations  1.29 us (2%)
    pallas_call x1, Pallas kernels, step(): pl.pallas_call(step_kernel, out_shape=[jax.ShapeDtypeStruct(*s) for s in...  46.1 us
    pallas_call x1, Pallas kernels, ocean_step(): pl.pallas_call(ocean_kernel, out_shape=[jax.ShapeDtypeStruct(*s) for s in...  5.49 us

profile of v2, /device:TPU:8, one launch (start us, length us, event | category | flops | bytes accessed | tf_op | source)
XLA Modules:
  0.0 52.9 jit_solution(11249541051999804543)
XLA Ops:
  1.3 46.1 %step.1 = (bf16[16,24,512]{2,1,0:T(8,128)(2,1)}, bf16[8,16,384]{2,1,0:T(8,128)(2,1)}, bf16[64,512]{1,0:T(8,128)(2,1)}, bf16[4,24,512]{2,1,0:T(8,128)(2,1)}, bf16...) custom-call(s32[1,3]{1,0:T(1,128)} %bitcast.14, s32[1,3]{1,0:T(1,128)} %bitcast.16, s32[1,1]{1,0:T(1,128)S(6)} %copy.24.count_ref, ...), custom_call_target="tpu_custom_call" | custom-call | tf_op jit(solution)/shard_map/step/pallas_call | solution.py:379
  47.4 5.5 %ocean.1 = (bf16[16,24,512]{2,1,0:T(8,128)(2,1)}, bf16[16,32,256]{2,1,0:T(8,128)(2,1)}) custom-call(s32[1,3]{1,0:T(1,128)} %bitcast.15, s32[1,3]{1,0:T(1,128)} %bitcast.17, s32[1,1]{1,0:T(1,128)S(6)} %copy.24.count_ref, bf16[8,16,384]{2,1,0:T(8,128)(2,1)} %get-tuple-element.8.fluxes_ref, f32[16,32,256]{2,1,0:T(8,128)} %get-tuple-element.9.conv_ref, ...), custom_call_target="tpu_custom_call" | custom-call | tf_op jit(solution)/shard_map/ocean/pallas_call | solution.py:477

commit v3 on v2

v3 whole, which is shorter than its diff:
```python
import types

import jax
import jax.numpy as jnp
from jax import lax
from jax.experimental import pallas as pl
from jax.experimental.pallas import tpu as pltpu
from jax.sharding import PartitionSpec as P

F32 = jnp.float32
BF16 = jnp.bfloat16
MESH = pl.DeviceIdType.MESH
HEADS = 16
HALF = 8
WIN = 8
NT = (((1,), (1,)), ((), ()))
TN = (((0,), (0,)), ((), ()))
NN = (((1,), (0,)), ((), ()))


def dot(a, b, dims):
    return lax.dot_general(a, b, dims, preferred_element_type=F32)


def iota(shape, dim):
    return lax.broadcasted_iota(jnp.int32, shape, dim)


def low_half(shape):
    return iota(shape, len(shape) - 2) % 8 < 4


def turn(x):
    return pltpu.roll(x, 4, x.ndim - 2)


def pack(x, high):
    n, _, lanes = x.shape
    x = x.reshape(n // 2, 2, 8, lanes)
    even, odd = x[:, 0], x[:, 1]
    if high:
        even = turn(even)
    else:
        odd = turn(odd)
    return jnp.where(low_half(even.shape), even, odd)


def unpack(x, high):
    n, _, lanes = x.shape
    other = turn(x)
    pair = (other, x) if high else (x, other)
    return jnp.stack(pair, axis=1).reshape(2 * n, 8, lanes)


def split2(x):
    top = x.astype(BF16).astype(F32)
    return top, x - top


def split3(x):
    top, rest = split2(x)
    middle, last = split2(rest)
    return top, middle, last


def greet(partners):
    barrier = pltpu.get_barrier_semaphore()
    for device in partners:
        pl.semaphore_signal(barrier, inc=1, device_id=device, device_id_type=MESH)
    return lambda: pl.semaphore_wait(barrier, len(partners))


def place():
    la, lo = lax.axis_index("lat"), lax.axis_index("lon")
    nla, nlo = lax.axis_size("lat"), lax.axis_size("lon")
    return lambda di, dj: (lax.rem(la + di + nla, nla), lax.rem(lo + dj + nlo, nlo))


def vmem(n):
    return [pl.BlockSpec(memory_space=pltpu.VMEM)] * n


def smem(n):
    return [pl.BlockSpec(memory_space=pltpu.SMEM)] * n


def anywhere(n):
    return [pl.BlockSpec(memory_space=pl.ANY)] * n


def layer_norm(x, gain, epsilon):
    average = jnp.mean(x, axis=-1, keepdims=True)
    centred = x - average
    spread = jnp.mean(centred * centred, axis=-1, keepdims=True)
    return centred * lax.rsqrt(spread + epsilon) * gain


def column_of(patch):
    p = patch.astype(F32)
    return p - 24.0 * jnp.floor((p + 0.5) * (1.0 / 24.0))


def mask_row(mask):
    wide = jnp.concatenate([mask.astype(F32), jnp.zeros((16, 96), F32)], axis=1)
    moved = [wide if q == 0 else pltpu.roll(wide, 32 * q, 1) for q in range(4)]
    parts = [sum(moved[q][4 * j + q : 4 * j + q + 1] for q in range(4)) for j in range(4)]
    return jnp.concatenate(parts, axis=1)


PARTNERS = [(0, 1), (0, -1), (0, 2), (0, -2), (1, 0), (-1, 0)]
COPIES = 32


def surface_message(owner_ref, block_ref, count_ref, ocean_ref, mask_ref, overlay_ref, proj_s, msg_s):
    lo = lax.axis_index("lon")
    nlo = lax.axis_size("lon")
    parts = jnp.concatenate(split3(proj_s[...]), axis=0).astype(BF16)
    surf = dot(parts, ocean_ref[...].reshape(512, 256), NT)
    surf = ((surf[0:8] + surf[8:16] + surf[16:24]) * mask_row(mask_ref[...])).astype(BF16)
    row = iota((8, 128), 0)
    twice = []
    codes = jnp.full((8, 128), -1.0, F32)
    for k in range(3):
        block = overlay_ref[k]
        twice.append(dot(surf, jnp.concatenate([block, block], axis=0), NT))
        side = lax.rem(owner_ref[0, k] - lo + 1 + nlo, nlo)
        code = jnp.where(k < count_ref[0, 0], side * 8 + block_ref[0, k], -1).astype(F32)
        codes = jnp.where(row == 4 + k, code, codes)
    msg_s[0:8] = jnp.where(row < 4, twice[0], twice[1])
    msg_s[8:16] = jnp.where(row < 4, twice[2], codes)


def gather_surface(msgs_ref):
    upper = iota((8, 128), 0) < 4
    right = iota((8, 128), 1) >= 64
    tiles = []
    for tile in range(2):
        sums = [jnp.zeros((8, 128), F32)] * 3
        for side in range(3):
            slot = tile - side + 2
            a = msgs_ref[slot, 0:8, :]
            b = msgs_ref[slot, 8:16, :]
            code_a = jnp.where(upper, b[4:5], b[5:6])
            code_b = jnp.where(upper, b[6:7], -1.0)
            for j in range(3):
                target = jnp.where(right, side * 8.0 + 2 * j + 1, side * 8.0 + 2 * j)
                sums[j] += jnp.where(code_a == target, a, 0.0) + jnp.where(code_b == target, b, 0.0)
        tiles.append(sums)
    return [
        jnp.where(column_of(iota((8, 128), 1) + 128 * j) < 4, tiles[1][j], tiles[0][j]) for j in range(3)
    ]


def bias_table(grid_ref, table_s, bias_s):
    grid = jnp.concatenate([grid_ref[...], jnp.zeros((16, 31), F32)], axis=1)
    for ra in range(8):
        rolled = grid if ra == 0 else pltpu.roll(grid, 256 - 15 * ra, 1)
        table_s[:, ra, :] = rolled[:, 0:128]
    parts = [x.astype(BF16) for x in split3(table_s[...].reshape(128, 128))]
    entry = iota((128, 64), 0)
    lane = iota((128, 64), 1)
    for ca in range(8):
        chosen = (entry == (7 - lane // 8) * 15 + ca - lane % 8 + 7).astype(BF16)
        found = (dot(parts[0], chosen, NN) + dot(parts[1], chosen, NN)) + dot(parts[2], chosen, NN)
        bias_s[:, ca, :] = found


def add_surface(sst, enc_s):
    s_hi, s_lo = split2(sst)
    e_hi, e_lo = split2(enc_s[...])
    left = jnp.concatenate([s_hi, s_lo, s_hi], axis=0).astype(BF16)
    right = jnp.concatenate([e_hi, e_hi, e_lo], axis=0).astype(BF16)
    return dot(left, right, TN)


def normalise(g, tokens, side, gain, mixed_s, norm_s):
    low = low_half((4, 8, 512))
    rows = slice(4 * g, 4 * g + 4)
    tokens = tokens.astype(F32)
    side = unpack(side.astype(F32).reshape(2, 8, 512), False)
    head = jnp.where(low, side, tokens[:, 0:8])
    tokens = jnp.concatenate([head, tokens[:, 8:24]], axis=1)
    mixed = (tokens + mixed_s[rows]).astype(BF16).astype(F32)
    mixed_s[rows] = mixed
    normed = layer_norm(mixed, gain, 1e-05)
    turned = [turn(normed[:, 8 * b : 8 * b + 8]) for b in range(3)]
    w_row, w_start = WINDOW_OF[g]
    for b in range(3):
        norm_s[w_row * 3 + b, w_start : w_start + 4] = jnp.where(low, turned[b], turned[(b + 1) % 3])


WINDOW_OF = ((1, 4), (0, 0), (0, 4), (1, 0))


def attend(w_row, norm_s, wqkv_s, bqkv_ref, wo_s, bias_s, last_s, q_s, k_s, v_s, att_s):
    rows = norm_s[3 * w_row : 3 * w_row + 3].reshape(192, 512).astype(BF16)
    for part, ref in enumerate((q_s, k_s, v_s)):
        cols = slice(512 * part, 512 * part + 512)
        value = dot(rows, wqkv_s[:, cols], NN) + bqkv_ref[cols].reshape(1, 512)
        if part == 0:
            value = value * 32 ** (-0.5)
        ref[...] = value.astype(BF16)
    own = (iota((8, 1, 256), 2) // 32) == iota((8, 1, 256), 0)

    def window(w, carry):
        at = pl.ds(pl.multiple_of(w * 64, 64), 64)
        for g in range(2):
            lanes = slice(256 * g, 256 * g + 256)
            queries = jnp.where(own, q_s[at, lanes][None], jnp.zeros((), BF16)).reshape(512, 256)
            scores = dot(queries, k_s[at, lanes], NT)
            scores = scores + bias_s[64 * g : 64 * g + 64].reshape(512, 64)
            if w_row == 1:
                scores = scores + last_s[...]
            scores = scores - jnp.max(scores, axis=-1, keepdims=True)
            weights = jnp.exp(scores)
            weights = (weights / jnp.sum(weights, axis=-1, keepdims=True)).astype(BF16)
            found = dot(weights, v_s[at, lanes], NN).reshape(8, 64, 256)
            att_s[at, lanes] = jnp.sum(jnp.where(own, found, 0.0), axis=0).astype(BF16)
        return carry

    lax.fori_loop(0, 3, window, 0)
    projected = dot(att_s[...], wo_s[...], NN).astype(BF16).astype(F32)
    norm_s[3 * w_row : 3 * w_row + 3] = projected.reshape(3, 8, 8, 512)


def finish(g, norm_s, mixed_s, cyc_ref, side_ref):
    w_row, w_start = WINDOW_OF[g]
    turned = [turn(norm_s[w_row * 3 + b, w_start : w_start + 4]) for b in range(3)]
    low = low_half((4, 8, 512))
    back = jnp.concatenate([jnp.where(low, turned[b - 1], turned[b]) for b in range(3)], axis=1)
    rows = slice(4 * g, 4 * g + 4)
    result = (mixed_s[rows] + back).astype(BF16)
    mixed_s[rows] = result.astype(F32)
    cyc_ref[rows] = result
    side_ref[...] = pack(result.astype(F32)[:, 0:8], False).reshape(16, 512).astype(BF16)


def convolve(pad_s, kernel_ref, cbias_ref, conv_ref):
    def band(i, carry):
        start = i * 8
        for h in range(2):
            lanes = slice(128 * h, 128 * h + 128)
            first_term = jnp.broadcast_to(cbias_ref[:, lanes], (8, 128))
            for b in range(4):
                sums = [first_term] * 8
                for v in range(7):
                    col = 8 * b + v + 5
                    cells = [pad_s[h, start + r, col : col + 8, :] for r in range(14)]
                    for u in range(7):
                        tap = kernel_ref[u, v : v + 1, lanes]
                        for r in range(8):
                            sums[r] = sums[r] + tap * cells[r + u]
                for r in range(8):
                    conv_ref[start + r, 8 * b : 8 * b + 8, lanes] = sums[r]
        return carry

    lax.fori_loop(0, 2, band, 0)


OPERANDS = (
    ("ocean", (16, 32, 256), BF16), ("proj", (4, 256), F32), ("mask", (16, 32), jnp.int32), ("overlay", (3, 64, 512), BF16),
    ("owner", (1, 3), jnp.int32), ("block", (1, 3), jnp.int32), ("count", (1, 1), jnp.int32), ("tok", (16, 24, 512), BF16),
    ("grid", (16, 225), F32), ("enc", (4, 512), F32), ("gain", (1, 512), F32), ("wqkv", (512, 1536), BF16),
    ("bqkv", (1536,), F32), ("wo", (512, 512), BF16), ("fp", (16, 512), BF16), ("kernel", (7, 7, 256), F32),
    ("cbias", (1, 256), F32), ("fenc", (16, 256), F32), ("ogain", (1, 256), F32), ("w1", (256, 1024), BF16),
    ("w2", (1024, 256), BF16), ("scale", (1, 256), F32),
)
SCALARS = ("owner", "block", "count")
SCRATCH = (
    ("proj8", (8, 256), F32), ("enc8", (8, 512), F32), ("msg", (16, 128), F32), ("msgs", (4, 16, 128), F32),
    ("side", (64, 512), BF16), ("east", (64, 512), BF16), ("south", (4, 24, 512), BF16), ("corner", (16, 512), BF16),
    ("sst", (8, 128), F32), ("under", (8, 128), F32), ("table", (16, 8, 128), F32), ("bias", (128, 8, 64), F32),
    ("last", (512, 64), F32), ("mixed", (16, 24, 512), F32), ("norm", (6, 8, 8, 512), F32), ("q", (192, 512), BF16),
    ("k", (192, 512), BF16), ("v", (192, 512), BF16), ("att", (192, 512), BF16), ("above", (3, 32, 256), BF16),
    ("below", (3, 32, 256), BF16), ("leave", (2, 88, 256), BF16), ("cols", (2, 88, 256), BF16),
    ("pad", (2, 22, 48, 128), F32), ("pe", (64, 512), BF16), ("flux", (16, 384), BF16), ("cyc", (16, 24, 512), BF16),
    ("fluxes", (8, 16, 384), BF16), ("west", (64, 512), BF16), ("north", (4, 24, 512), BF16), ("nw", (16, 512), BF16),
    ("conv", (16, 32, 256), F32), ("pre", (512, 256), F32), ("rate", (512, 256), F32), ("atm", (16, 24, 512), BF16),
    ("out", (16, 32, 256), BF16),
)


def pick_flux(x, codes):
    lane = iota((16, 128), 1)
    right = lane >= 64
    picked = [jnp.zeros((16, 128), F32)] * 3
    for j in range(3):
        patch = lane + 128 * j
        east = column_of(patch) < 4
        south = patch < 96
        at = slice(128 * j, 128 * j + 128)
        for side in range(3):
            here = jnp.where(east, x.fluxes[side, :, at].astype(F32), x.fluxes[side + 1, :, at].astype(F32))
            under = jnp.where(east, x.fluxes[4 + side, :, at].astype(F32), x.fluxes[5 + side, :, at].astype(F32))
            tile = jnp.where(south, under, here)
            target = jnp.where(right, side * 8 + 2 * j + 1, side * 8 + 2 * j)
            for k in range(3):
                picked[k] += jnp.where(target == codes[k], tile, 0.0)
    picked = [y + pltpu.roll(y, 64, 1) for y in picked]
    return jnp.concatenate([jnp.where(right, picked[1], picked[0]), picked[2][:, 0:64]], axis=1)


def slot_codes(x):
    lo = lax.axis_index("lon")
    nlo = lax.axis_size("lon")
    codes = []
    for k in range(3):
        side = lax.rem(x.owner[0, k] - lo + 1 + nlo, nlo)
        codes.append(jnp.where(k < x.count[0, 0], side * 8 + x.block[0, k], -1))
    return codes


def ocean_rate(x):
    mask = jnp.broadcast_to(mask_row(x.mask[...]), (16, 512)).astype(BF16)
    parts = [jnp.broadcast_to(y, (16, 256)) for y in split3(x.scale[...])]
    row = iota((16, 256), 0)
    scale = jnp.where(row == 0, parts[0], jnp.where(row == 1, parts[1], jnp.where(row == 2, parts[2], 0.0)))
    x.rate[...] = dot(mask, scale.astype(BF16), TN)


def ocean_update(x):
    forcing = dot(pick_flux(x, slot_codes(x)).astype(BF16), x.overlay[...].reshape(192, 512), NN)
    f_hi, f_lo = split2(forcing)
    e_hi, e_lo = split2(x.fenc[...])
    x.pre[...] = x.conv[...].reshape(512, 256) + dot(
        jnp.concatenate([f_hi, f_lo, f_hi], axis=0).astype(BF16),
        jnp.concatenate([e_hi, e_hi, e_lo], axis=0).astype(BF16),
        TN,
    )

    def cells(i, carry):
        at = pl.ds(pl.multiple_of(i * 128, 128), 128)
        normed = layer_norm(x.pre[at], x.ogain[...], 1e-06).astype(BF16)
        update = jnp.zeros((128, 256), F32)
        for c in range(4):
            cols = slice(256 * c, 256 * c + 256)
            y = dot(normed, x.w1[:, cols], NN)
            hidden = (0.5 * y * (1.0 + lax.erf(y * (0.5**0.5)))).astype(BF16)
            update = update + dot(hidden, x.w2[cols], NN)
        rows = pl.ds(i * 4, 4)
        state = x.ocean[rows].astype(F32).reshape(128, 256)
        x.out[rows] = (state + x.rate[at] * update).astype(BF16).reshape(4, 32, 256)
        return carry

    lax.fori_loop(0, 4, cells, 0)


def assemble(g, x):
    low = low_half((4, 8, 512))
    rows = slice(4 * g, 4 * g + 4)
    body, side = (x.north, x.nw[...]) if g == 0 else (x.cyc.at[rows], x.west[16 * g : 16 * g + 16])
    body = body[...].astype(F32)
    side = unpack(side.astype(F32).reshape(2, 8, 512), False)
    head = jnp.where(low, side, body[:, 0:8])
    x.atm[rows] = jnp.concatenate([head, body[:, 8:24]], axis=1).astype(BF16)


def step_kernel(*refs):
    n = len(OPERANDS)
    given = dict(zip([o[0] for o in OPERANDS], refs[:n]))
    atm_ref, out_ref = refs[n : n + 2]
    refs = refs[n + 2 :]
    x = types.SimpleNamespace(**dict(zip([o[0] for o in (*OPERANDS, *SCRATCH)], refs)))
    load_sem, store_sem, send_sem, recv_sem = refs[n + len(SCRATCH) :]

    at = place()
    la = lax.axis_index("lat")
    nla = lax.axis_size("lat")
    wait_barrier = greet([at(*o) for o in PARTNERS])
    loads = {}
    for i, (name, *_) in enumerate(OPERANDS):
        loads[name] = pltpu.make_async_copy(given[name], getattr(x, name), load_sem.at[i])
        loads[name].start()

    def loaded(*names):
        for name in names:
            loads[name].wait()

    copies = []

    def send(src, dst, offset):
        i = len(copies)
        copy = pltpu.make_async_remote_copy(
            src_ref=src, dst_ref=dst, send_sem=send_sem.at[i], recv_sem=recv_sem.at[i],
            device_id=at(*offset), device_id_type=MESH,
        )
        copies.append(copy)
        copy.start()
        return copy

    loaded("ocean", "proj", "mask", "overlay", "owner", "block", "count")
    for half in range(2):
        x.proj8[4 * half : 4 * half + 4] = x.proj[...]
    surface_message(x.owner, x.block, x.count, x.ocean, x.mask, x.overlay, x.proj8, x.msg)
    loaded("tok")
    x.side[...] = pack(x.tok[:, 0:8, :].astype(F32), False).reshape(64, 512).astype(BF16)

    wait_barrier()
    messages = [send(x.msg, x.msgs.at[dj + 1], (0, -dj)) for dj in (2, 1, -1)]
    x.msgs[1] = x.msg[...]
    east_top = send(x.side.at[pl.ds(0, 16)], x.east.at[pl.ds(0, 16)], (0, -1))
    east = send(x.side.at[pl.ds(16, 48)], x.east.at[pl.ds(16, 48)], (0, -1))
    south = send(x.tok.at[pl.ds(0, 4)], x.south, (-1, 0))

    loaded("grid", "enc", "gain")
    for half in range(2):
        x.enc8[4 * half : 4 * half + 4] = x.enc[...]
    bias_table(x.grid, x.table, x.bias)
    edge = la == nla - 1
    a_row = (iota((512, 64), 0) % 64) >= 32
    b_row = iota((512, 64), 1) >= 32
    x.last[...] = jnp.where(edge, jnp.where(a_row != b_row, -1e9, 0.0), 0.0)

    for copy in messages:
        copy.wait_recv()
    sst = gather_surface(x.msgs)
    x.sst[...] = sst[0]
    under = send(x.sst, x.under, (-1, 0))
    east_top.wait_recv()
    corner = send(x.east.at[pl.ds(0, 16)], x.corner, (-1, 0))
    below = send(x.ocean.at[pl.ds(0, 3)], x.below, (-1, 0))
    above = send(x.ocean.at[pl.ds(13, 3)], x.above, (1, 0))
    x.mixed[...] = add_surface(jnp.concatenate(sst, axis=1), x.enc8).reshape(16, 24, 512)
    gain = x.gain[...].reshape(1, 1, 512)
    east.wait_recv()
    for g in (1, 2, 3):
        normalise(g, x.tok[4 * g : 4 * g + 4], x.east[16 * g : 16 * g + 16], gain, x.mixed, x.norm)
    loaded("wqkv", "bqkv", "wo")
    windows = (x.norm, x.wqkv, x.bqkv, x.wo, x.bias, x.last, x.q, x.k, x.v, x.att)
    attend(0, *windows)
    for g in (1, 2):
        finish(g, x.norm, x.mixed, x.cyc, x.pe.at[pl.ds(16 * g, 16)])
    pieces = [send(x.pe.at[pl.ds(16, 32)], x.west.at[pl.ds(16, 32)], (0, 1))]

    def put(rows, cols, values):
        for h in range(2):
            x.pad[h, rows, cols, :] = values[:, :, 128 * h : 128 * h + 128]

    below.wait_recv()
    above.wait_recv()
    put(slice(3, 19), slice(8, 40), x.ocean[...].astype(F32))
    put(slice(0, 3), slice(8, 40), x.above[...].astype(F32) * (la > 0).astype(F32))
    put(slice(19, 22), slice(8, 40), x.below[...].astype(F32) * (la < nla - 1).astype(F32))
    for h in range(2):
        lanes = slice(128 * h, 128 * h + 128)
        x.leave[0, :, lanes] = pack(x.pad[h, :, 32:40, :], True).reshape(88, 128).astype(BF16)
        x.leave[1, :, lanes] = pack(x.pad[h, :, 8:16, :], False).reshape(88, 128).astype(BF16)
    sides = [send(x.leave.at[0], x.cols.at[0], (0, 1)), send(x.leave.at[1], x.cols.at[1], (0, -1))]
    loaded("scale")
    ocean_rate(x)

    for copy in (under, south, corner):
        copy.wait_recv()
    x.mixed[0:4] = add_surface(x.under[...], x.enc8)[0:96].reshape(4, 24, 512)
    normalise(0, x.south[...], x.corner[...], gain, x.mixed, x.norm)
    attend(1, *windows)
    for g in (3, 0):
        finish(g, x.norm, x.mixed, x.cyc, x.pe.at[pl.ds(16 * g, 16)])
    loaded("fp")
    x.flux[...] = dot(x.fp[...], x.mixed[...].reshape(384, 512).astype(BF16), NT).astype(BF16)
    fluxes = [
        send(x.flux, x.fluxes.at[down * 4 + dj + 2], (down, -dj))
        for down in (1, 0) for dj in (1, -2, -1, 0) if (down, dj) != (0, 0)
    ]
    pieces += [
        send(x.pe.at[pl.ds(48, 16)], x.west.at[pl.ds(48, 16)], (0, 1)),
        send(x.pe.at[pl.ds(0, 16)], x.nw, (1, 1)),
        send(x.cyc.at[pl.ds(0, 4)], x.north, (1, 0)),
    ]
    x.fluxes[2] = x.flux[...]

    for copy in sides:
        copy.wait_recv()
    for side, high in ((0, True), (1, False)):
        values = unpack(x.cols[side].astype(F32).reshape(11, 8, 256), high)
        put(slice(0, 22), slice(40 * side, 40 * side + 8), values)
    loaded("kernel", "cbias")
    convolve(x.pad, x.kernel, x.cbias, x.conv)

    loaded("fenc", "ogain", "w1", "w2")
    for copy in fluxes:
        copy.wait_recv()
    ocean_update(x)
    stores = [pltpu.make_async_copy(x.out, out_ref, store_sem.at[0])]
    stores[0].start()
    for copy in pieces:
        copy.wait_recv()
    for g in range(4):
        assemble(g, x)
    stores.append(pltpu.make_async_copy(x.atm, atm_ref, store_sem.at[1]))
    stores[1].start()
    for copy in copies:
        copy.wait_send()
    for copy in stores:
        copy.wait()


def step(*operands):
    def copy_of(name, shape, kind):
        return pltpu.SMEM(shape, kind) if name in SCALARS else pltpu.VMEM(shape, kind)

    shapes = [((16, 24, 512), BF16), ((16, 32, 256), BF16)]
    return pl.pallas_call(
        step_kernel,
        out_shape=[jax.ShapeDtypeStruct(*s) for s in shapes],
        in_specs=anywhere(len(OPERANDS)),
        out_specs=anywhere(len(shapes)),
        scratch_shapes=[
            *[copy_of(*o) for o in (*OPERANDS, *SCRATCH)],
            pltpu.SemaphoreType.DMA((len(OPERANDS),)), pltpu.SemaphoreType.DMA((2,)),
            pltpu.SemaphoreType.DMA((COPIES,)), pltpu.SemaphoreType.DMA((COPIES,)),
        ],
        compiler_params=pltpu.CompilerParams(collective_id=0, has_side_effects=True),
        name="step",
    )(*operands)


def local(
    atmos_patch_tokens,
    atmos_norm_gain,
    query_key_value_weight,
    query_key_value_bias,
    relative_bias_grid,
    attention_output_weight,
    flux_projector,
    surface_encoder,
    ocean_cell_state,
    land_sea_mask,
    depthwise_conv_kernel,
    depthwise_conv_bias,
    ocean_norm_gain,
    pointwise_expand,
    pointwise_contract,
    layer_update_scale,
    forcing_encoder,
    surface_projector,
    overlay_area_weight,
    owners,
    owner_tile_blocks,
    counts,
):
    owners = owners.reshape(1, 3)
    blocks = owner_tile_blocks.reshape(1, 3)
    overlay = overlay_area_weight.reshape(3, 64, 512)
    atm_out, ocean_out = step(
        ocean_cell_state, surface_projector.T, land_sea_mask, overlay, owners, blocks, counts, atmos_patch_tokens,
        relative_bias_grid, surface_encoder, atmos_norm_gain.reshape(1, 512), query_key_value_weight, query_key_value_bias,
        attention_output_weight, flux_projector.T, depthwise_conv_kernel, depthwise_conv_bias.reshape(1, 256), forcing_encoder,
        ocean_norm_gain.reshape(1, 256), pointwise_expand, pointwise_contract, layer_update_scale.reshape(1, 256),
    )
    return atm_out, ocean_out


def solution(mesh):
    rep = P()
    placed = (
        P("lat", "lon", None), rep, rep, rep, rep, rep, rep, rep, P("lat", "lon", None), P("lat", "lon"),
        rep, rep, rep, rep, rep, rep, rep, rep, P("lat", "lon", None, None, None),
        P("lat", "lon", None), P("lat", "lon", None), P("lat", "lon"),
    )
    return jax.shard_map(
        local,
        mesh=mesh,
        in_specs=placed,
        out_specs=(P("lat", "lon", None), P("lat", "lon", None)),
        check_vma=False,
    )
```

time: 53.1 us -> 51.9 us (0.977)
  the two profiles are of different devices: /device:TPU:8 before, /device:TPU:1 now
where the time goes in v3:
time: 51.9 us; the launch traced here: 51.7 us
  Pallas kernels  46.9 us (90%)
  local copies, waits for them, and re-layouts  3.44 us (7%)
  between operations  1.29 us (2%)
    pallas_call x1, Pallas kernels, step(): pl.pallas_call(step_kernel, out_shape=[jax.ShapeDtypeStruct(*s) for s in...  46.9 us
    unnamed x2, local copies, waits for them, and re-layouts  3.44 us

profile of v3, /device:TPU:1, one launch (start us, length us, event | category | flops | bytes accessed | tf_op | source)
XLA Modules:
  0.0 51.7 jit_solution(17110278749608456451)
XLA Ops:
  1.3 46.9 %step.1 = (bf16[16,24,512]{2,1,0:T(8,128)(2,1)}, bf16[16,32,256]{2,1,0:T(8,128)(2,1)}) custom-call(bf16[16,32,256]{2,1,0:T(8,128)(2,1)} %refs_0_.1, f32[4,256]{1,0:T(4,128)} %bitcast.11, s32[16,32]{1,0:T(8,128)} %refs_2_.1, bf16[3,64,512]{2,1,0:T(8,128)(2,1)} %bitcast.9, s32[1,3]{1,0:T(1,128)} %bitcast.16, s32[1,3]{1,0:T(1,128)} %bitcast.17, ...), custom_call_target="tpu_custom_call" | custom-call | tf_op jit(solution)/shard_map/step/pallas_call | solution.py:503
  48.2 1.8 %copy.27 = bf16[16,24,512]{2,1,0:T(8,128)(2,1)} copy(bf16[16,24,512]{2,1,0:T(8,128)(2,1)} %get-tuple-element.4) | data formatting | bytes 786432
  50.0 1.7 %copy.28 = bf16[16,32,256]{2,1,0:T(8,128)(2,1)} copy(bf16[16,32,256]{2,1,0:T(8,128)(2,1)} %get-tuple-element.5) | data formatting | bytes 524288

commit v4 on v3

--- a/solution.py
+++ b/solution.py
@@ -273,9 +273,11 @@
     ("last", (512, 64), F32), ("mixed", (16, 24, 512), F32), ("norm", (6, 8, 8, 512), F32), ("q", (192, 512), BF16),
     ("k", (192, 512), BF16), ("v", (192, 512), BF16), ("att", (192, 512), BF16), ("above", (3, 32, 256), BF16),
     ("below", (3, 32, 256), BF16), ("leave", (2, 88, 256), BF16), ("cols", (2, 88, 256), BF16),
-    ("pad", (2, 22, 48, 128), F32), ("pe", (64, 512), BF16), ("flux", (16, 384), BF16), ("cyc", (16, 24, 512), BF16),
-    ("fluxes", (8, 16, 384), BF16), ("west", (64, 512), BF16), ("north", (4, 24, 512), BF16), ("nw", (16, 512), BF16),
-    ("conv", (16, 32, 256), F32), ("pre", (512, 256), F32), ("rate", (512, 256), F32), ("atm", (16, 24, 512), BF16),
+    ("pad", (2, 22, 48, 128), F32), ("pe", (64, 512), BF16), ("flux", (16, 384), BF16),
+    ("fluxes", (8, 16, 384), BF16), ("conv", (16, 32, 256), F32), ("pre", (512, 256), F32), ("rate", (512, 256), F32),
+)
+RESULTS = (
+    ("cyc", (16, 24, 512), BF16), ("west", (64, 512), BF16), ("north", (4, 24, 512), BF16), ("nw", (16, 512), BF16),
     ("out", (16, 32, 256), BF16),
 )
 
@@ -358,10 +360,9 @@
 def step_kernel(*refs):
     n = len(OPERANDS)
     given = dict(zip([o[0] for o in OPERANDS], refs[:n]))
-    atm_ref, out_ref = refs[n : n + 2]
-    refs = refs[n + 2 :]
-    x = types.SimpleNamespace(**dict(zip([o[0] for o in (*OPERANDS, *SCRATCH)], refs)))
-    load_sem, store_sem, send_sem, recv_sem = refs[n + len(SCRATCH) :]
+    names = [o[0] for o in (*RESULTS, *OPERANDS, *SCRATCH)]
+    x = types.SimpleNamespace(**dict(zip(names, refs[n:])))
+    load_sem, send_sem, recv_sem = refs[n + len(names) :]
 
     at = place()
     la = lax.axis_index("lat")
@@ -395,7 +396,8 @@
     loaded("tok")
     x.side[...] = pack(x.tok[:, 0:8, :].astype(F32), False).reshape(64, 512).astype(BF16)
 
-    wait_barrier()
+    with jax.named_scope("w_barrier"):
+        wait_barrier()
     messages = [send(x.msg, x.msgs.at[dj + 1], (0, -dj)) for dj in (2, 1, -1)]
     x.msgs[1] = x.msg[...]
     east_top = send(x.side.at[pl.ds(0, 16)], x.east.at[pl.ds(0, 16)], (0, -1))
@@ -411,18 +413,21 @@
     b_row = iota((512, 64), 1) >= 32
     x.last[...] = jnp.where(edge, jnp.where(a_row != b_row, -1e9, 0.0), 0.0)
 
-    for copy in messages:
-        copy.wait_recv()
+    with jax.named_scope("w_messages"):
+        for copy in messages:
+            copy.wait_recv()
     sst = gather_surface(x.msgs)
     x.sst[...] = sst[0]
     under = send(x.sst, x.under, (-1, 0))
-    east_top.wait_recv()
+    with jax.named_scope("w_top"):
+        east_top.wait_recv()
     corner = send(x.east.at[pl.ds(0, 16)], x.corner, (-1, 0))
     below = send(x.ocean.at[pl.ds(0, 3)], x.below, (-1, 0))
     above = send(x.ocean.at[pl.ds(13, 3)], x.above, (1, 0))
     x.mixed[...] = add_surface(jnp.concatenate(sst, axis=1), x.enc8).reshape(16, 24, 512)
     gain = x.gain[...].reshape(1, 1, 512)
-    east.wait_recv()
+    with jax.named_scope("w_east"):
+        east.wait_recv()
     for g in (1, 2, 3):
         normalise(g, x.tok[4 * g : 4 * g + 4], x.east[16 * g : 16 * g + 16], gain, x.mixed, x.norm)
     loaded("wqkv", "bqkv", "wo")
@@ -436,8 +441,9 @@
         for h in range(2):
             x.pad[h, rows, cols, :] = values[:, :, 128 * h : 128 * h + 128]
 
-    below.wait_recv()
-    above.wait_recv()
+    with jax.named_scope("w_rows"):
+        below.wait_recv()
+        above.wait_recv()
     put(slice(3, 19), slice(8, 40), x.ocean[...].astype(F32))
     put(slice(0, 3), slice(8, 40), x.above[...].astype(F32) * (la > 0).astype(F32))
     put(slice(19, 22), slice(8, 40), x.below[...].astype(F32) * (la < nla - 1).astype(F32))
@@ -449,8 +455,11 @@
     loaded("scale")
     ocean_rate(x)
 
-    for copy in (under, south, corner):
-        copy.wait_recv()
+    with jax.named_scope("w_under"):
+        under.wait_recv()
+    with jax.named_scope("w_south"):
+        south.wait_recv()
+        corner.wait_recv()
     x.mixed[0:4] = add_surface(x.under[...], x.enc8)[0:96].reshape(4, 24, 512)
     normalise(0, x.south[...], x.corner[...], gain, x.mixed, x.norm)
     attend(1, *windows)
@@ -469,8 +478,9 @@
     ]
     x.fluxes[2] = x.flux[...]
 
-    for copy in sides:
-        copy.wait_recv()
+    with jax.named_scope("w_sides"):
+        for copy in sides:
+            copy.wait_recv()
     for side, high in ((0, True), (1, False)):
         values = unpack(x.cols[side].astype(F32).reshape(11, 8, 256), high)
         put(slice(0, 22), slice(40 * side, 40 * side + 8), values)
@@ -478,37 +488,55 @@
     convolve(x.pad, x.kernel, x.cbias, x.conv)
 
     loaded("fenc", "ogain", "w1", "w2")
-    for copy in fluxes:
-        copy.wait_recv()
+    with jax.named_scope("w_flux"):
+        for copy in fluxes:
+            copy.wait_recv()
     ocean_update(x)
-    stores = [pltpu.make_async_copy(x.out, out_ref, store_sem.at[0])]
+    with jax.named_scope("w_pieces"):
+        for copy in pieces:
+            copy.wait_recv()
+        for copy in copies:
+            copy.wait_send()
+
+
+def last_kernel(cyc_ref, west_ref, north_ref, nw_ref, out_ref, atm_to, out_to, atm_s, store_sem):
+    stores = [pltpu.make_async_copy(out_ref, out_to, store_sem.at[0])]
     stores[0].start()
-    for copy in pieces:
-        copy.wait_recv()
+    x = types.SimpleNamespace(cyc=cyc_ref, west=west_ref, north=north_ref, nw=nw_ref, atm=atm_s)
     for g in range(4):
         assemble(g, x)
-    stores.append(pltpu.make_async_copy(x.atm, atm_ref, store_sem.at[1]))
-    stores[1].start()
-    for copy in copies:
-        copy.wait_send()
+        rows = pl.ds(4 * g, 4)
+        stores.append(pltpu.make_async_copy(atm_s.at[rows], atm_to.at[rows], store_sem.at[g + 1]))
+        stores[-1].start()
     for copy in stores:
         copy.wait()
+
+
+def last(*results):
+    shapes = [((16, 24, 512), BF16), ((16, 32, 256), BF16)]
+    return pl.pallas_call(
+        last_kernel,
+        out_shape=[jax.ShapeDtypeStruct(*s) for s in shapes],
+        in_specs=vmem(len(results)),
+        out_specs=anywhere(len(shapes)),
+        scratch_shapes=[pltpu.VMEM((16, 24, 512), BF16), pltpu.SemaphoreType.DMA((5,))],
+        compiler_params=pltpu.CompilerParams(vmem_limit_bytes=24 << 20),
+        name="last",
+    )(*results)
 
 
 def step(*operands):
     def copy_of(name, shape, kind):
         return pltpu.SMEM(shape, kind) if name in SCALARS else pltpu.VMEM(shape, kind)
 
-    shapes = [((16, 24, 512), BF16), ((16, 32, 256), BF16)]
     return pl.pallas_call(
         step_kernel,
-        out_shape=[jax.ShapeDtypeStruct(*s) for s in shapes],
-        in_specs=anywhere(len(OPERANDS)),
-        out_specs=anywhere(len(shapes)),
+        out_shape=[pltpu.VMEM(shape, kind) for _, shape, kind in RESULTS],
+        in_specs=[pl.BlockSpec(memory_space=pltpu.HBM)] * len(OPERANDS),
+        out_specs=vmem(len(RESULTS)),
         scratch_shapes=[
             *[copy_of(*o) for o in (*OPERANDS, *SCRATCH)],
-            pltpu.SemaphoreType.DMA((len(OPERANDS),)), pltpu.SemaphoreType.DMA((2,)),
-            pltpu.SemaphoreType.DMA((COPIES,)), pltpu.SemaphoreType.DMA((COPIES,)),
+            pltpu.SemaphoreType.DMA((len(OPERANDS),)), pltpu.SemaphoreType.DMA((COPIES,)), pltpu.SemaphoreType.DMA((COPIES,)),
         ],
         compiler_params=pltpu.CompilerParams(collective_id=0, has_side_effects=True),
         name="step",
@@ -542,13 +570,13 @@
     owners = owners.reshape(1, 3)
     blocks = owner_tile_blocks.reshape(1, 3)
     overlay = overlay_area_weight.reshape(3, 64, 512)
-    atm_out, ocean_out = step(
+    results = step(
         ocean_cell_state, surface_projector.T, land_sea_mask, overlay, owners, blocks, counts, atmos_patch_tokens,
         relative_bias_grid, surface_encoder, atmos_norm_gain.reshape(1, 512), query_key_value_weight, query_key_value_bias,
         attention_output_weight, flux_projector.T, depthwise_conv_kernel, depthwise_conv_bias.reshape(1, 256), forcing_encoder,
         ocean_norm_gain.reshape(1, 256), pointwise_expand, pointwise_contract, layer_update_scale.reshape(1, 256),
     )
-    return atm_out, ocean_out
+    return last(*results)
 
 
 def solution(mesh):

time: 51.9 us -> 48.1 us (0.927)
  local copies, waits for them, and re-layouts: 3.44 us -> 0 us
    unnamed x2 -> x0, local copies, waits for them, and re-layouts: 3.44 us -> none
    pallas_call x1 -> x2, Pallas kernels: 46.9 us -> 46.7 us  [the longest x1 45.8 us: step(): pl.pallas_call(step_kernel, out_shape=[pltpu.VMEM(shape, kind) for _, sha...]
where the time goes in v4:
time: 48.1 us; the launch traced here: 48 us
  Pallas kernels  46.7 us (97%)
  between operations  1.29 us (3%)
    pallas_call x1, Pallas kernels, step(): pl.pallas_call(step_kernel, out_shape=[pltpu.VMEM(shape, kind) for _, sha...  45.8 us

profile of v4, /device:TPU:1, one launch (start us, length us, event | category | flops | bytes accessed | tf_op | source)
XLA Modules:
  0.0 48.0 jit_solution(14135132280723350299)
XLA Ops:
  1.3 45.8 %step.1 = (bf16[16,24,512]{2,1,0:T(8,128)(2,1)S(1)}, bf16[64,512]{1,0:T(8,128)(2,1)S(1)}, bf16[4,24,512]{2,1,0:T(8,128)(2,1)S(1)}, bf16[16,512]{1,0:T(8,128)(2,1)S(1)}, bf16[16,32,256]{2,1,0:T(8,128)(2,1)S(1)}) custom-call(bf16[16,32,256]{2,1,0:T(8,128)(2,1)} %refs_0_.1, f32[4,256]{1,0:T(4,128)} %bitcast.11, s32[16,32]{1,0:T(8,128)} %refs_2_.1, ...), custom_call_target="tpu_custom_call" | custom-call | tf_op jit(solution)/shard_map/step/pallas_call | solution.py:532
  47.1 0.9 %last.1 = (bf16[16,24,512]{2,1,0:T(8,128)(2,1)}, bf16[16,32,256]{2,1,0:T(8,128)(2,1)}) custom-call(bf16[16,24,512]{2,1,0:T(8,128)(2,1)S(1)} %get-tuple-element.7.cyc_ref, bf16[64,512]{1,0:T(8,128)(2,1)S(1)} %get-tuple-element.8.west_ref, bf16[4,24,512]{2,1,0:T(8,128)(2,1)S(1)} %get-tuple-element.9.north_ref, bf16[16,512]{1,0:T(8,128)(2,1)S(1)} %get-tuple-element.10.nw_ref, ...), custom_call_target="tpu_custom_call" | custom-call | tf_op jit(solution)/shard_map/last/pallas_call | solution.py:517

commit v5 on v4

--- a/solution.py
+++ b/solution.py
@@ -151,7 +151,7 @@
     ]
 
 
-def bias_table(grid_ref, table_s, bias_s):
+def bias_table(grid_ref, table_s, rows_s, bias_s):
     grid = jnp.concatenate([grid_ref[...], jnp.zeros((16, 31), F32)], axis=1)
     for ra in range(8):
         rolled = grid if ra == 0 else pltpu.roll(grid, 256 - 15 * ra, 1)
@@ -162,7 +162,10 @@
     for ca in range(8):
         chosen = (entry == (7 - lane // 8) * 15 + ca - lane % 8 + 7).astype(BF16)
         found = (dot(parts[0], chosen, NN) + dot(parts[1], chosen, NN)) + dot(parts[2], chosen, NN)
-        bias_s[:, ca, :] = found
+        rows_s[:, ca, :] = found
+    for part in range(8):
+        rows = rows_s[16 * part : 16 * part + 16].reshape(128, 64)
+        bias_s[:, 128 * part : 128 * part + 128] = rows.T
 
 
 def add_surface(sst, enc_s):
@@ -201,24 +204,23 @@
             value = value * 32 ** (-0.5)
         ref[...] = value.astype(BF16)
     own = (iota((8, 1, 256), 2) // 32) == iota((8, 1, 256), 0)
-
-    def window(w, carry):
-        at = pl.ds(pl.multiple_of(w * 64, 64), 64)
+    first_head = iota((64, 128), 0) < 32
+    for w in range(3):
+        at = slice(64 * w, 64 * w + 64)
         for g in range(2):
             lanes = slice(256 * g, 256 * g + 256)
             queries = jnp.where(own, q_s[at, lanes][None], jnp.zeros((), BF16)).reshape(512, 256)
-            scores = dot(queries, k_s[at, lanes], NT)
-            scores = scores + bias_s[64 * g : 64 * g + 64].reshape(512, 64)
+            scores = dot(k_s[at, lanes], queries, NT) + bias_s[:, 512 * g : 512 * g + 512]
             if w_row == 1:
                 scores = scores + last_s[...]
-            scores = scores - jnp.max(scores, axis=-1, keepdims=True)
-            weights = jnp.exp(scores)
-            weights = (weights / jnp.sum(weights, axis=-1, keepdims=True)).astype(BF16)
-            found = dot(weights, v_s[at, lanes], NN).reshape(8, 64, 256)
-            att_s[at, lanes] = jnp.sum(jnp.where(own, found, 0.0), axis=0).astype(BF16)
-        return carry
-
-    lax.fori_loop(0, 3, window, 0)
+            scores = jnp.exp(scores - jnp.max(scores, axis=0, keepdims=True))
+            weights = (scores * (1.0 / jnp.sum(scores, axis=0, keepdims=True))).astype(BF16)
+            values = v_s[at, lanes].astype(F32).T.astype(BF16)
+            found = []
+            for pair in range(4):
+                both = dot(values[64 * pair : 64 * pair + 64], weights[:, 128 * pair : 128 * pair + 128], NN)
+                found.append(jnp.where(first_head, both, pltpu.roll(both, 64, 1)))
+            att_s[at, lanes] = jnp.concatenate(found, axis=0).T[0:64].astype(BF16)
     projected = dot(att_s[...], wo_s[...], NN).astype(BF16).astype(F32)
     norm_s[3 * w_row : 3 * w_row + 3] = projected.reshape(3, 8, 8, 512)
 
@@ -269,12 +271,13 @@
 SCRATCH = (
     ("proj8", (8, 256), F32), ("enc8", (8, 512), F32), ("msg", (16, 128), F32), ("msgs", (4, 16, 128), F32),
     ("side", (64, 512), BF16), ("east", (64, 512), BF16), ("south", (4, 24, 512), BF16), ("corner", (16, 512), BF16),
-    ("sst", (8, 128), F32), ("under", (8, 128), F32), ("table", (16, 8, 128), F32), ("bias", (128, 8, 64), F32),
-    ("last", (512, 64), F32), ("mixed", (16, 24, 512), F32), ("norm", (6, 8, 8, 512), F32), ("q", (192, 512), BF16),
+    ("sst", (8, 128), F32), ("under", (8, 128), F32), ("table", (16, 8, 128), F32), ("rows", (128, 8, 64), F32),
+    ("bias", (64, 1024), F32), ("last", (64, 512), F32), ("mixed", (16, 24, 512), F32), ("norm", (6, 8, 8, 512), F32), ("q", (192, 512), BF16),
     ("k", (192, 512), BF16), ("v", (192, 512), BF16), ("att", (192, 512), BF16), ("above", (3, 32, 256), BF16),
     ("below", (3, 32, 256), BF16), ("leave", (2, 88, 256), BF16), ("cols", (2, 88, 256), BF16),
     ("pad", (2, 22, 48, 128), F32), ("pe", (64, 512), BF16), ("flux", (16, 384), BF16),
-    ("fluxes", (8, 16, 384), BF16), ("conv", (16, 32, 256), F32), ("pre", (512, 256), F32), ("rate", (512, 256), F32),
+    ("near", (2, 16, 384), BF16), ("top", (16, 128), BF16), ("rim", (16, 128), BF16),
+    ("tops", (3, 16, 128), BF16), ("edge", (2, 16, 128), BF16), ("spread", (64, 384), BF16), ("conv", (16, 32, 256), F32), ("pre", (512, 256), F32), ("rate", (512, 256), F32),
 )
 RESULTS = (
     ("cyc", (16, 24, 512), BF16), ("west", (64, 512), BF16), ("north", (4, 24, 512), BF16), ("nw", (16, 512), BF16),
@@ -282,19 +285,28 @@
 )
 
 
+def spread(x):
+    patch = iota((64, 384), 0)
+    x.spread[...] = (iota((64, 384), 1) == 24 * (patch // 4) + patch % 4).astype(BF16)
+
+
 def pick_flux(x, codes):
     lane = iota((16, 128), 1)
     right = lane >= 64
+    edge = dot(x.edge[...].reshape(32, 128)[:, 0:64], x.spread[...], NN)
+    west, own, east = x.near[0].astype(F32), x.flux[...].astype(F32), x.near[1].astype(F32)
+    heads, bodies = (edge[0:16], west, own), (west, own, east)
+    tops = [x.tops[n].astype(F32) for n in range(3)]
+    top_heads = (edge[16:32, 0:128], tops[0], tops[1])
     picked = [jnp.zeros((16, 128), F32)] * 3
     for j in range(3):
         patch = lane + 128 * j
-        east = column_of(patch) < 4
-        south = patch < 96
+        head = column_of(patch) < 4
         at = slice(128 * j, 128 * j + 128)
         for side in range(3):
-            here = jnp.where(east, x.fluxes[side, :, at].astype(F32), x.fluxes[side + 1, :, at].astype(F32))
-            under = jnp.where(east, x.fluxes[4 + side, :, at].astype(F32), x.fluxes[5 + side, :, at].astype(F32))
-            tile = jnp.where(south, under, here)
+            tile = jnp.where(head, heads[side][:, at], bodies[side][:, at])
+            if j == 0:
+                tile = jnp.where(patch < 96, jnp.where(head, top_heads[side], tops[side]), tile)
             target = jnp.where(right, side * 8 + 2 * j + 1, side * 8 + 2 * j)
             for k in range(3):
                 picked[k] += jnp.where(target == codes[k], tile, 0.0)
@@ -396,8 +408,7 @@
     loaded("tok")
     x.side[...] = pack(x.tok[:, 0:8, :].astype(F32), False).reshape(64, 512).astype(BF16)
 
-    with jax.named_scope("w_barrier"):
-        wait_barrier()
+    wait_barrier()
     messages = [send(x.msg, x.msgs.at[dj + 1], (0, -dj)) for dj in (2, 1, -1)]
     x.msgs[1] = x.msg[...]
     east_top = send(x.side.at[pl.ds(0, 16)], x.east.at[pl.ds(0, 16)], (0, -1))
@@ -407,27 +418,24 @@
     loaded("grid", "enc", "gain")
     for half in range(2):
         x.enc8[4 * half : 4 * half + 4] = x.enc[...]
-    bias_table(x.grid, x.table, x.bias)
+    bias_table(x.grid, x.table, x.rows, x.bias)
     edge = la == nla - 1
-    a_row = (iota((512, 64), 0) % 64) >= 32
-    b_row = iota((512, 64), 1) >= 32
+    a_row = (iota((64, 512), 1) % 64) >= 32
+    b_row = iota((64, 512), 0) >= 32
     x.last[...] = jnp.where(edge, jnp.where(a_row != b_row, -1e9, 0.0), 0.0)
 
-    with jax.named_scope("w_messages"):
-        for copy in messages:
-            copy.wait_recv()
+    for copy in messages:
+        copy.wait_recv()
     sst = gather_surface(x.msgs)
     x.sst[...] = sst[0]
     under = send(x.sst, x.under, (-1, 0))
-    with jax.named_scope("w_top"):
-        east_top.wait_recv()
+    east_top.wait_recv()
     corner = send(x.east.at[pl.ds(0, 16)], x.corner, (-1, 0))
     below = send(x.ocean.at[pl.ds(0, 3)], x.below, (-1, 0))
     above = send(x.ocean.at[pl.ds(13, 3)], x.above, (1, 0))
     x.mixed[...] = add_surface(jnp.concatenate(sst, axis=1), x.enc8).reshape(16, 24, 512)
     gain = x.gain[...].reshape(1, 1, 512)
-    with jax.named_scope("w_east"):
-        east.wait_recv()
+    east.wait_recv()
     for g in (1, 2, 3):
         normalise(g, x.tok[4 * g : 4 * g + 4], x.east[16 * g : 16 * g + 16], gain, x.mixed, x.norm)
     loaded("wqkv", "bqkv", "wo")
@@ -441,9 +449,8 @@
         for h in range(2):
             x.pad[h, rows, cols, :] = values[:, :, 128 * h : 128 * h + 128]
 
-    with jax.named_scope("w_rows"):
-        below.wait_recv()
-        above.wait_recv()
+    below.wait_recv()
+    above.wait_recv()
     put(slice(3, 19), slice(8, 40), x.ocean[...].astype(F32))
     put(slice(0, 3), slice(8, 40), x.above[...].astype(F32) * (la > 0).astype(F32))
     put(slice(19, 22), slice(8, 40), x.below[...].astype(F32) * (la < nla - 1).astype(F32))
@@ -454,33 +461,39 @@
     sides = [send(x.leave.at[0], x.cols.at[0], (0, 1)), send(x.leave.at[1], x.cols.at[1], (0, -1))]
     loaded("scale")
     ocean_rate(x)
-
-    with jax.named_scope("w_under"):
-        under.wait_recv()
-    with jax.named_scope("w_south"):
-        south.wait_recv()
-        corner.wait_recv()
+    spread(x)
+
+    under.wait_recv()
+    south.wait_recv()
+    corner.wait_recv()
     x.mixed[0:4] = add_surface(x.under[...], x.enc8)[0:96].reshape(4, 24, 512)
     normalise(0, x.south[...], x.corner[...], gain, x.mixed, x.norm)
     attend(1, *windows)
     for g in (3, 0):
         finish(g, x.norm, x.mixed, x.cyc, x.pe.at[pl.ds(16 * g, 16)])
     loaded("fp")
-    x.flux[...] = dot(x.fp[...], x.mixed[...].reshape(384, 512).astype(BF16), NT).astype(BF16)
+    flux = dot(x.fp[...], x.mixed[...].reshape(384, 512).astype(BF16), NT).astype(BF16)
+    x.flux[...] = flux
+    x.top[...] = flux[:, 0:128]
+    edge = dot(x.fp[...], x.pe[...], NT)
+    x.rim[...] = jnp.concatenate([edge, jnp.zeros((16, 64), F32)], axis=1).astype(BF16)
     fluxes = [
-        send(x.flux, x.fluxes.at[down * 4 + dj + 2], (down, -dj))
-        for down in (1, 0) for dj in (1, -2, -1, 0) if (down, dj) != (0, 0)
+        send(x.top, x.tops.at[2], (1, -1)),
+        send(x.rim, x.edge.at[1], (1, 2)),
+        send(x.rim, x.edge.at[0], (0, 2)),
+        send(x.top, x.tops.at[0], (1, 1)),
+        send(x.top, x.tops.at[1], (1, 0)),
+        send(x.flux, x.near.at[1], (0, -1)),
+        send(x.flux, x.near.at[0], (0, 1)),
     ]
     pieces += [
         send(x.pe.at[pl.ds(48, 16)], x.west.at[pl.ds(48, 16)], (0, 1)),
         send(x.pe.at[pl.ds(0, 16)], x.nw, (1, 1)),
         send(x.cyc.at[pl.ds(0, 4)], x.north, (1, 0)),
     ]
-    x.fluxes[2] = x.flux[...]
-
-    with jax.named_scope("w_sides"):
-        for copy in sides:
-            copy.wait_recv()
+
+    for copy in sides:
+        copy.wait_recv()
     for side, high in ((0, True), (1, False)):
         values = unpack(x.cols[side].astype(F32).reshape(11, 8, 256), high)
         put(slice(0, 22), slice(40 * side, 40 * side + 8), values)
@@ -488,15 +501,13 @@
     convolve(x.pad, x.kernel, x.cbias, x.conv)
 
     loaded("fenc", "ogain", "w1", "w2")
-    with jax.named_scope("w_flux"):
-        for copy in fluxes:
-            copy.wait_recv()
+    for copy in fluxes:
+        copy.wait_recv()
     ocean_update(x)
-    with jax.named_scope("w_pieces"):
-        for copy in pieces:
-            copy.wait_recv()
-        for copy in copies:
-            copy.wait_send()
+    for copy in pieces:
+        copy.wait_recv()
+    for copy in copies:
+        copy.wait_send()
 
 
 def last_kernel(cyc_ref, west_ref, north_ref, nw_ref, out_ref, atm_to, out_to, atm_s, store_sem):

time: 48.1 us -> 44.1 us (0.917)
  Pallas kernels: 46.7 us -> 42.7 us
    pallas_call x1, Pallas kernels: 45.8 us -> 41.8 us  [step(): pl.pallas_call(step_kernel, out_shape=[pltpu.VMEM(shape, kind) for _, sha...]
where the time goes in v5:
time: 44.1 us; the launch traced here: 44 us
  Pallas kernels  42.7 us (97%)
  between operations  1.29 us (3%)
    pallas_call x1, Pallas kernels, step(): pl.pallas_call(step_kernel, out_shape=[pltpu.VMEM(shape, kind) for _, sha...  41.8 us

profile of v5, /device:TPU:1, one launch (start us, length us, event | category | flops | bytes accessed | tf_op | source)
XLA Modules:
  0.0 44.0 jit_solution(6328869406374231325)
XLA Ops:
  1.3 41.8 %step.1 = (bf16[16,24,512]{2,1,0:T(8,128)(2,1)S(1)}, bf16[64,512]{1,0:T(8,128)(2,1)S(1)}, bf16[4,24,512]{2,1,0:T(8,128)(2,1)S(1)}, bf16[16,512]{1,0:T(8,128)(2,1)S(1)}, bf16[16,32,256]{2,1,0:T(8,128)(2,1)S(1)}) custom-call(bf16[16,32,256]{2,1,0:T(8,128)(2,1)} %refs_0_.1, f32[4,256]{1,0:T(4,128)} %bitcast.11, s32[16,32]{1,0:T(8,128)} %refs_2_.1, ...), custom_call_target="tpu_custom_call" | custom-call | tf_op jit(solution)/shard_map/step/pallas_call | solution.py:543
  43.1 0.9 %last.1 = (bf16[16,24,512]{2,1,0:T(8,128)(2,1)}, bf16[16,32,256]{2,1,0:T(8,128)(2,1)}) custom-call(bf16[16,24,512]{2,1,0:T(8,128)(2,1)S(1)} %get-tuple-element.7.cyc_ref, bf16[64,512]{1,0:T(8,128)(2,1)S(1)} %get-tuple-element.8.west_ref, bf16[4,24,512]{2,1,0:T(8,128)(2,1)S(1)} %get-tuple-element.9.north_ref, bf16[16,512]{1,0:T(8,128)(2,1)S(1)} %get-tuple-element.10.nw_ref, ...), custom_call_target="tpu_custom_call" | custom-call | tf_op jit(solution)/shard_map/last/pallas_call | solution.py:528

commit v6 on v5

--- a/solution.py
+++ b/solution.py
@@ -270,8 +270,8 @@
 SCALARS = ("owner", "block", "count")
 SCRATCH = (
     ("proj8", (8, 256), F32), ("enc8", (8, 512), F32), ("msg", (16, 128), F32), ("msgs", (4, 16, 128), F32),
-    ("side", (64, 512), BF16), ("east", (64, 512), BF16), ("south", (4, 24, 512), BF16), ("corner", (16, 512), BF16),
-    ("sst", (8, 128), F32), ("under", (8, 128), F32), ("table", (16, 8, 128), F32), ("rows", (128, 8, 64), F32),
+    ("side", (64, 512), BF16), ("east", (64, 512), BF16), ("upper", (4, 24, 512), BF16), ("corner", (16, 512), BF16),
+    ("sst", (8, 128), F32), ("over", (8, 128), F32), ("table", (16, 8, 128), F32), ("rows", (128, 8, 64), F32),
     ("bias", (64, 1024), F32), ("last", (64, 512), F32), ("mixed", (16, 24, 512), F32), ("norm", (6, 8, 8, 512), F32), ("q", (192, 512), BF16),
     ("k", (192, 512), BF16), ("v", (192, 512), BF16), ("att", (192, 512), BF16), ("above", (3, 32, 256), BF16),
     ("below", (3, 32, 256), BF16), ("leave", (2, 88, 256), BF16), ("cols", (2, 88, 256), BF16),
@@ -280,7 +280,7 @@
     ("tops", (3, 16, 128), BF16), ("edge", (2, 16, 128), BF16), ("spread", (64, 384), BF16), ("conv", (16, 32, 256), F32), ("pre", (512, 256), F32), ("rate", (512, 256), F32),
 )
 RESULTS = (
-    ("cyc", (16, 24, 512), BF16), ("west", (64, 512), BF16), ("north", (4, 24, 512), BF16), ("nw", (16, 512), BF16),
+    ("cyc", (16, 24, 512), BF16), ("west", (64, 512), BF16), ("south", (4, 24, 512), BF16), ("sw", (16, 512), BF16),
     ("out", (16, 32, 256), BF16),
 )
 
@@ -297,7 +297,7 @@
     west, own, east = x.near[0].astype(F32), x.flux[...].astype(F32), x.near[1].astype(F32)
     heads, bodies = (edge[0:16], west, own), (west, own, east)
     tops = [x.tops[n].astype(F32) for n in range(3)]
-    top_heads = (edge[16:32, 0:128], tops[0], tops[1])
+    top_heads = (edge[16:32, 256:384], tops[0], tops[1])
     picked = [jnp.zeros((16, 128), F32)] * 3
     for j in range(3):
         patch = lane + 128 * j
@@ -305,8 +305,8 @@
         at = slice(128 * j, 128 * j + 128)
         for side in range(3):
             tile = jnp.where(head, heads[side][:, at], bodies[side][:, at])
-            if j == 0:
-                tile = jnp.where(patch < 96, jnp.where(head, top_heads[side], tops[side]), tile)
+            if j == 2:
+                tile = jnp.where(patch >= 288, jnp.where(head, top_heads[side], tops[side]), tile)
             target = jnp.where(right, side * 8 + 2 * j + 1, side * 8 + 2 * j)
             for k in range(3):
                 picked[k] += jnp.where(target == codes[k], tile, 0.0)
@@ -342,8 +342,8 @@
         TN,
     )
 
-    def cells(i, carry):
-        at = pl.ds(pl.multiple_of(i * 128, 128), 128)
+    for i in range(4):
+        at = slice(128 * i, 128 * i + 128)
         normed = layer_norm(x.pre[at], x.ogain[...], 1e-06).astype(BF16)
         update = jnp.zeros((128, 256), F32)
         for c in range(4):
@@ -351,18 +351,15 @@
             y = dot(normed, x.w1[:, cols], NN)
             hidden = (0.5 * y * (1.0 + lax.erf(y * (0.5**0.5)))).astype(BF16)
             update = update + dot(hidden, x.w2[cols], NN)
-        rows = pl.ds(i * 4, 4)
+        rows = slice(4 * i, 4 * i + 4)
         state = x.ocean[rows].astype(F32).reshape(128, 256)
         x.out[rows] = (state + x.rate[at] * update).astype(BF16).reshape(4, 32, 256)
-        return carry
-
-    lax.fori_loop(0, 4, cells, 0)
 
 
 def assemble(g, x):
     low = low_half((4, 8, 512))
     rows = slice(4 * g, 4 * g + 4)
-    body, side = (x.north, x.nw[...]) if g == 0 else (x.cyc.at[rows], x.west[16 * g : 16 * g + 16])
+    body, side = (x.south, x.sw[...]) if g == 3 else (x.cyc.at[rows], x.west[16 * g : 16 * g + 16])
     body = body[...].astype(F32)
     side = unpack(side.astype(F32).reshape(2, 8, 512), False)
     head = jnp.where(low, side, body[:, 0:8])
@@ -411,15 +408,15 @@
     wait_barrier()
     messages = [send(x.msg, x.msgs.at[dj + 1], (0, -dj)) for dj in (2, 1, -1)]
     x.msgs[1] = x.msg[...]
-    east_top = send(x.side.at[pl.ds(0, 16)], x.east.at[pl.ds(0, 16)], (0, -1))
-    east = send(x.side.at[pl.ds(16, 48)], x.east.at[pl.ds(16, 48)], (0, -1))
-    south = send(x.tok.at[pl.ds(0, 4)], x.south, (-1, 0))
+    east_end = send(x.side.at[pl.ds(48, 16)], x.east.at[pl.ds(48, 16)], (0, -1))
+    east = send(x.side.at[pl.ds(0, 48)], x.east.at[pl.ds(0, 48)], (0, -1))
+    upper = send(x.tok.at[pl.ds(12, 4)], x.upper, (1, 0))
 
     loaded("grid", "enc", "gain")
     for half in range(2):
         x.enc8[4 * half : 4 * half + 4] = x.enc[...]
     bias_table(x.grid, x.table, x.rows, x.bias)
-    edge = la == nla - 1
+    edge = la == 0
     a_row = (iota((64, 512), 1) % 64) >= 32
     b_row = iota((64, 512), 0) >= 32
     x.last[...] = jnp.where(edge, jnp.where(a_row != b_row, -1e9, 0.0), 0.0)
@@ -427,16 +424,16 @@
     for copy in messages:
         copy.wait_recv()
     sst = gather_surface(x.msgs)
-    x.sst[...] = sst[0]
-    under = send(x.sst, x.under, (-1, 0))
-    east_top.wait_recv()
-    corner = send(x.east.at[pl.ds(0, 16)], x.corner, (-1, 0))
+    x.sst[...] = sst[2]
+    over = send(x.sst, x.over, (1, 0))
+    east_end.wait_recv()
+    corner = send(x.east.at[pl.ds(48, 16)], x.corner, (1, 0))
     below = send(x.ocean.at[pl.ds(0, 3)], x.below, (-1, 0))
     above = send(x.ocean.at[pl.ds(13, 3)], x.above, (1, 0))
     x.mixed[...] = add_surface(jnp.concatenate(sst, axis=1), x.enc8).reshape(16, 24, 512)
     gain = x.gain[...].reshape(1, 1, 512)
     east.wait_recv()
-    for g in (1, 2, 3):
+    for g in (1, 2, 0):
         normalise(g, x.tok[4 * g : 4 * g + 4], x.east[16 * g : 16 * g + 16], gain, x.mixed, x.norm)
     loaded("wqkv", "bqkv", "wo")
     windows = (x.norm, x.wqkv, x.bqkv, x.wo, x.bias, x.last, x.q, x.k, x.v, x.att)
@@ -463,33 +460,32 @@
     ocean_rate(x)
     spread(x)
 
-    under.wait_recv()
-    south.wait_recv()
-    corner.wait_recv()
-    x.mixed[0:4] = add_surface(x.under[...], x.enc8)[0:96].reshape(4, 24, 512)
-    normalise(0, x.south[...], x.corner[...], gain, x.mixed, x.norm)
+    for copy in (over, upper, corner):
+        copy.wait_recv()
+    x.mixed[12:16] = add_surface(x.over[...], x.enc8)[32:128].reshape(4, 24, 512)
+    normalise(3, x.upper[...], x.corner[...], gain, x.mixed, x.norm)
     attend(1, *windows)
     for g in (3, 0):
         finish(g, x.norm, x.mixed, x.cyc, x.pe.at[pl.ds(16 * g, 16)])
     loaded("fp")
     flux = dot(x.fp[...], x.mixed[...].reshape(384, 512).astype(BF16), NT).astype(BF16)
     x.flux[...] = flux
-    x.top[...] = flux[:, 0:128]
+    x.top[...] = flux[:, 256:384]
     edge = dot(x.fp[...], x.pe[...], NT)
     x.rim[...] = jnp.concatenate([edge, jnp.zeros((16, 64), F32)], axis=1).astype(BF16)
     fluxes = [
-        send(x.top, x.tops.at[2], (1, -1)),
-        send(x.rim, x.edge.at[1], (1, 2)),
+        send(x.top, x.tops.at[0], (-1, 1)),
+        send(x.rim, x.edge.at[1], (-1, 2)),
         send(x.rim, x.edge.at[0], (0, 2)),
-        send(x.top, x.tops.at[0], (1, 1)),
-        send(x.top, x.tops.at[1], (1, 0)),
+        send(x.top, x.tops.at[2], (-1, -1)),
+        send(x.top, x.tops.at[1], (-1, 0)),
         send(x.flux, x.near.at[1], (0, -1)),
         send(x.flux, x.near.at[0], (0, 1)),
     ]
     pieces += [
-        send(x.pe.at[pl.ds(48, 16)], x.west.at[pl.ds(48, 16)], (0, 1)),
-        send(x.pe.at[pl.ds(0, 16)], x.nw, (1, 1)),
-        send(x.cyc.at[pl.ds(0, 4)], x.north, (1, 0)),
+        send(x.pe.at[pl.ds(0, 16)], x.west.at[pl.ds(0, 16)], (0, 1)),
+        send(x.pe.at[pl.ds(48, 16)], x.sw, (-1, 1)),
+        send(x.cyc.at[pl.ds(12, 4)], x.south, (-1, 0)),
     ]
 
     for copy in sides:
@@ -510,10 +506,10 @@
         copy.wait_send()
 
 
-def last_kernel(cyc_ref, west_ref, north_ref, nw_ref, out_ref, atm_to, out_to, atm_s, store_sem):
+def last_kernel(cyc_ref, west_ref, south_ref, sw_ref, out_ref, atm_to, out_to, atm_s, store_sem):
     stores = [pltpu.make_async_copy(out_ref, out_to, store_sem.at[0])]
     stores[0].start()
-    x = types.SimpleNamespace(cyc=cyc_ref, west=west_ref, north=north_ref, nw=nw_ref, atm=atm_s)
+    x = types.SimpleNamespace(cyc=cyc_ref, west=west_ref, south=south_ref, sw=sw_ref, atm=atm_s)
     for g in range(4):
         assemble(g, x)
         rows = pl.ds(4 * g, 4)

time: 44.1 us -> 43.8 us (level)
  the two profiles are of different devices: /device:TPU:1 before, /device:TPU:48 now
where the time goes in v6:
time: 43.8 us; the launch traced here: 43.6 us
  Pallas kernels  42.4 us (97%)
  between operations  1.29 us (3%)
    pallas_call x1, Pallas kernels, step(): pl.pallas_call(step_kernel, out_shape=[pltpu.VMEM(shape, kind) for _, sha...  41.5 us

profile of v6, /device:TPU:48, one launch (start us, length us, event | category | flops | bytes accessed | tf_op | source)
XLA Modules:
  0.0 43.6 jit_solution(169980655048818257)
XLA Ops:
  1.3 41.5 %step.1 = (bf16[16,24,512]{2,1,0:T(8,128)(2,1)S(1)}, bf16[64,512]{1,0:T(8,128)(2,1)S(1)}, bf16[4,24,512]{2,1,0:T(8,128)(2,1)S(1)}, bf16[16,512]{1,0:T(8,128)(2,1)S(1)}, bf16[16,32,256]{2,1,0:T(8,128)(2,1)S(1)}) custom-call(bf16[16,32,256]{2,1,0:T(8,128)(2,1)} %refs_0_.1, f32[4,256]{1,0:T(4,128)} %bitcast.11, s32[16,32]{1,0:T(8,128)} %refs_2_.1, ...), custom_call_target="tpu_custom_call" | custom-call | tf_op jit(solution)/shard_map/step/pallas_call | solution.py:539
  42.8 0.9 %last.1 = (bf16[16,24,512]{2,1,0:T(8,128)(2,1)}, bf16[16,32,256]{2,1,0:T(8,128)(2,1)}) custom-call(bf16[16,24,512]{2,1,0:T(8,128)(2,1)S(1)} %get-tuple-element.7.cyc_ref, bf16[64,512]{1,0:T(8,128)(2,1)S(1)} %get-tuple-element.8.west_ref, bf16[4,24,512]{2,1,0:T(8,128)(2,1)S(1)} %get-tuple-element.9.south_ref, bf16[16,512]{1,0:T(8,128)(2,1)S(1)} %get-tuple-element.10.sw_ref, ...), custom_call_target="tpu_custom_call" | custom-call | tf_op jit(solution)/shard_map/last/pallas_call | solution.py:524

commit v7 on v6

--- a/solution.py
+++ b/solution.py
@@ -411,6 +411,8 @@
     east_end = send(x.side.at[pl.ds(48, 16)], x.east.at[pl.ds(48, 16)], (0, -1))
     east = send(x.side.at[pl.ds(0, 48)], x.east.at[pl.ds(0, 48)], (0, -1))
     upper = send(x.tok.at[pl.ds(12, 4)], x.upper, (1, 0))
+    above = send(x.ocean.at[pl.ds(13, 3)], x.above, (1, 0))
+    below = send(x.ocean.at[pl.ds(0, 3)], x.below, (-1, 0))
 
     loaded("grid", "enc", "gain")
     for half in range(2):
@@ -428,8 +430,6 @@
     over = send(x.sst, x.over, (1, 0))
     east_end.wait_recv()
     corner = send(x.east.at[pl.ds(48, 16)], x.corner, (1, 0))
-    below = send(x.ocean.at[pl.ds(0, 3)], x.below, (-1, 0))
-    above = send(x.ocean.at[pl.ds(13, 3)], x.above, (1, 0))
     x.mixed[...] = add_surface(jnp.concatenate(sst, axis=1), x.enc8).reshape(16, 24, 512)
     gain = x.gain[...].reshape(1, 1, 512)
     east.wait_recv()
@@ -440,7 +440,6 @@
     attend(0, *windows)
     for g in (1, 2):
         finish(g, x.norm, x.mixed, x.cyc, x.pe.at[pl.ds(16 * g, 16)])
-    pieces = [send(x.pe.at[pl.ds(16, 32)], x.west.at[pl.ds(16, 32)], (0, 1))]
 
     def put(rows, cols, values):
         for h in range(2):
@@ -482,8 +481,8 @@
         send(x.flux, x.near.at[1], (0, -1)),
         send(x.flux, x.near.at[0], (0, 1)),
     ]
-    pieces += [
-        send(x.pe.at[pl.ds(0, 16)], x.west.at[pl.ds(0, 16)], (0, 1)),
+    pieces = [
+        send(x.pe.at[pl.ds(0, 48)], x.west.at[pl.ds(0, 48)], (0, 1)),
         send(x.pe.at[pl.ds(48, 16)], x.sw, (-1, 1)),
         send(x.cyc.at[pl.ds(12, 4)], x.south, (-1, 0)),
     ]

time: 43.8 us -> 43.7 us (level)
  the two profiles are of different devices: /device:TPU:48 before, /device:TPU:32 now
where the time goes in v7:
time: 43.7 us; the launch traced here: 43.6 us
  Pallas kernels  42.3 us (97%)
  between operations  1.29 us (3%)
    pallas_call x1, Pallas kernels, step(): pl.pallas_call(step_kernel, out_shape=[pltpu.VMEM(shape, kind) for _, sha...  41.4 us

profile of v7, /device:TPU:32, one launch (start us, length us, event | category | flops | bytes accessed | tf_op | source)
XLA Modules:
  0.0 43.6 jit_solution(2884215565373387488)
XLA Ops:
  1.3 41.4 %step.1 = (bf16[16,24,512]{2,1,0:T(8,128)(2,1)S(1)}, bf16[64,512]{1,0:T(8,128)(2,1)S(1)}, bf16[4,24,512]{2,1,0:T(8,128)(2,1)S(1)}, bf16[16,512]{1,0:T(8,128)(2,1)S(1)}, bf16[16,32,256]{2,1,0:T(8,128)(2,1)S(1)}) custom-call(bf16[16,32,256]{2,1,0:T(8,128)(2,1)} %refs_0_.1, f32[4,256]{1,0:T(4,128)} %bitcast.11, s32[16,32]{1,0:T(8,128)} %refs_2_.1, ...), custom_call_target="tpu_custom_call" | custom-call | tf_op jit(solution)/shard_map/step/pallas_call | solution.py:538
  42.7 0.9 %last.1 = (bf16[16,24,512]{2,1,0:T(8,128)(2,1)}, bf16[16,32,256]{2,1,0:T(8,128)(2,1)}) custom-call(bf16[16,24,512]{2,1,0:T(8,128)(2,1)S(1)} %get-tuple-element.7.cyc_ref, bf16[64,512]{1,0:T(8,128)(2,1)S(1)} %get-tuple-element.8.west_ref, bf16[4,24,512]{2,1,0:T(8,128)(2,1)S(1)} %get-tuple-element.9.south_ref, bf16[16,512]{1,0:T(8,128)(2,1)S(1)} %get-tuple-element.10.sw_ref, ...), custom_call_target="tpu_custom_call" | custom-call | tf_op jit(solution)/shard_map/last/pallas_call | solution.py:523

commit v8 on v7

--- a/solution.py
+++ b/solution.py
@@ -423,6 +423,9 @@
     b_row = iota((64, 512), 0) >= 32
     x.last[...] = jnp.where(edge, jnp.where(a_row != b_row, -1e9, 0.0), 0.0)
 
+    loaded("scale")
+    ocean_rate(x)
+    spread(x)
     for copy in messages:
         copy.wait_recv()
     sst = gather_surface(x.msgs)
@@ -433,7 +436,7 @@
     x.mixed[...] = add_surface(jnp.concatenate(sst, axis=1), x.enc8).reshape(16, 24, 512)
     gain = x.gain[...].reshape(1, 1, 512)
     east.wait_recv()
-    for g in (1, 2, 0):
+    for g in (1, 2):
         normalise(g, x.tok[4 * g : 4 * g + 4], x.east[16 * g : 16 * g + 16], gain, x.mixed, x.norm)
     loaded("wqkv", "bqkv", "wo")
     windows = (x.norm, x.wqkv, x.bqkv, x.wo, x.bias, x.last, x.q, x.k, x.v, x.att)
@@ -455,9 +458,8 @@
         x.leave[0, :, lanes] = pack(x.pad[h, :, 32:40, :], True).reshape(88, 128).astype(BF16)
         x.leave[1, :, lanes] = pack(x.pad[h, :, 8:16, :], False).reshape(88, 128).astype(BF16)
     sides = [send(x.leave.at[0], x.cols.at[0], (0, 1)), send(x.leave.at[1], x.cols.at[1], (0, -1))]
-    loaded("scale")
-    ocean_rate(x)
-    spread(x)
+    pieces = [send(x.pe.at[pl.ds(16, 32)], x.west.at[pl.ds(16, 32)], (0, 1))]
+    normalise(0, x.tok[0:4], x.east[0:16], gain, x.mixed, x.norm)
 
     for copy in (over, upper, corner):
         copy.wait_recv()
@@ -481,8 +483,8 @@
         send(x.flux, x.near.at[1], (0, -1)),
         send(x.flux, x.near.at[0], (0, 1)),
     ]
-    pieces = [
-        send(x.pe.at[pl.ds(0, 48)], x.west.at[pl.ds(0, 48)], (0, 1)),
+    pieces += [
+        send(x.pe.at[pl.ds(0, 16)], x.west.at[pl.ds(0, 16)], (0, 1)),
         send(x.pe.at[pl.ds(48, 16)], x.sw, (-1, 1)),
         send(x.cyc.at[pl.ds(12, 4)], x.south, (-1, 0)),
     ]

time: 43.7 us -> 42.4 us (0.970)
  the two profiles are of different devices: /device:TPU:32 before, /device:TPU:40 now
where the time goes in v8:
time: 42.4 us; the launch traced here: 42.3 us
  Pallas kernels  41 us (97%)
  between operations  1.29 us (3%)
    pallas_call x1, Pallas kernels, step(): pl.pallas_call(step_kernel, out_shape=[pltpu.VMEM(shape, kind) for _, sha...  40.1 us
    pallas_call x1, Pallas kernels, last(): pl.pallas_call(last_kernel, out_shape=[jax.ShapeDtypeStruct(*s) for s in...  0.87 us

profile of v8, /device:TPU:40, one launch (start us, length us, event | category | flops | bytes accessed | tf_op | source)
XLA Modules:
  0.0 42.3 jit_solution(3463591451826470646)
XLA Ops:
  1.3 40.1 %step.1 = (bf16[16,24,512]{2,1,0:T(8,128)(2,1)S(1)}, bf16[64,512]{1,0:T(8,128)(2,1)S(1)}, bf16[4,24,512]{2,1,0:T(8,128)(2,1)S(1)}, bf16[16,512]{1,0:T(8,128)(2,1)S(1)}, bf16[16,32,256]{2,1,0:T(8,128)(2,1)S(1)}) custom-call(bf16[16,32,256]{2,1,0:T(8,128)(2,1)} %refs_0_.1, f32[4,256]{1,0:T(4,128)} %bitcast.11, s32[16,32]{1,0:T(8,128)} %refs_2_.1, ...), custom_call_target="tpu_custom_call" | custom-call | tf_op jit(solution)/shard_map/step/pallas_call | solution.py:540
  41.4 0.9 %last.1 = (bf16[16,24,512]{2,1,0:T(8,128)(2,1)}, bf16[16,32,256]{2,1,0:T(8,128)(2,1)}) custom-call(bf16[16,24,512]{2,1,0:T(8,128)(2,1)S(1)} %get-tuple-element.7.cyc_ref, bf16[64,512]{1,0:T(8,128)(2,1)S(1)} %get-tuple-element.8.west_ref, bf16[4,24,512]{2,1,0:T(8,128)(2,1)S(1)} %get-tuple-element.9.south_ref, bf16[16,512]{1,0:T(8,128)(2,1)S(1)} %get-tuple-element.10.sw_ref, ...), custom_call_target="tpu_custom_call" | custom-call | tf_op jit(solution)/shard_map/last/pallas_call | solution.py:525

commit v9 on v8

--- a/solution.py
+++ b/solution.py
@@ -433,6 +433,20 @@
     over = send(x.sst, x.over, (1, 0))
     east_end.wait_recv()
     corner = send(x.east.at[pl.ds(48, 16)], x.corner, (1, 0))
+    def put(rows, cols, values):
+        for h in range(2):
+            x.pad[h, rows, cols, :] = values[:, :, 128 * h : 128 * h + 128]
+
+    below.wait_recv()
+    above.wait_recv()
+    put(slice(3, 19), slice(8, 40), x.ocean[...].astype(F32))
+    put(slice(0, 3), slice(8, 40), x.above[...].astype(F32) * (la > 0).astype(F32))
+    put(slice(19, 22), slice(8, 40), x.below[...].astype(F32) * (la < nla - 1).astype(F32))
+    for h in range(2):
+        lanes = slice(128 * h, 128 * h + 128)
+        x.leave[0, :, lanes] = pack(x.pad[h, :, 32:40, :], True).reshape(88, 128).astype(BF16)
+        x.leave[1, :, lanes] = pack(x.pad[h, :, 8:16, :], False).reshape(88, 128).astype(BF16)
+    sides = [send(x.leave.at[0], x.cols.at[0], (0, 1)), send(x.leave.at[1], x.cols.at[1], (0, -1))]
     x.mixed[...] = add_surface(jnp.concatenate(sst, axis=1), x.enc8).reshape(16, 24, 512)
     gain = x.gain[...].reshape(1, 1, 512)
     east.wait_recv()
@@ -444,20 +458,6 @@
     for g in (1, 2):
         finish(g, x.norm, x.mixed, x.cyc, x.pe.at[pl.ds(16 * g, 16)])
 
-    def put(rows, cols, values):
-        for h in range(2):
-            x.pad[h, rows, cols, :] = values[:, :, 128 * h : 128 * h + 128]
-
-    below.wait_recv()
-    above.wait_recv()
-    put(slice(3, 19), slice(8, 40), x.ocean[...].astype(F32))
-    put(slice(0, 3), slice(8, 40), x.above[...].astype(F32) * (la > 0).astype(F32))
-    put(slice(19, 22), slice(8, 40), x.below[...].astype(F32) * (la < nla - 1).astype(F32))
-    for h in range(2):
-        lanes = slice(128 * h, 128 * h + 128)
-        x.leave[0, :, lanes] = pack(x.pad[h, :, 32:40, :], True).reshape(88, 128).astype(BF16)
-        x.leave[1, :, lanes] = pack(x.pad[h, :, 8:16, :], False).reshape(88, 128).astype(BF16)
-    sides = [send(x.leave.at[0], x.cols.at[0], (0, 1)), send(x.leave.at[1], x.cols.at[1], (0, -1))]
     pieces = [send(x.pe.at[pl.ds(16, 32)], x.west.at[pl.ds(16, 32)], (0, 1))]
     normalise(0, x.tok[0:4], x.east[0:16], gain, x.mixed, x.norm)
 

time: 42.4 us -> 41.8 us (0.986)
  the two profiles are of different devices: /device:TPU:40 before, /device:TPU:1 now
where the time goes in v9:
time: 41.8 us; the launch traced here: 41.1 us
  Pallas kernels  39.8 us (95%)
  between operations  1.29 us (3%)
    pallas_call x1, Pallas kernels, step(): pl.pallas_call(step_kernel, out_shape=[pltpu.VMEM(shape, kind) for _, sha...  38.9 us
    pallas_call x1, Pallas kernels, last(): pl.pallas_call(last_kernel, out_shape=[jax.ShapeDtypeStruct(*s) for s in...  0.87 us

profile of v9, /device:TPU:1, one launch (start us, length us, event | category | flops | bytes accessed | tf_op | source)
XLA Modules:
  0.0 41.1 jit_solution(1310746947203446189)
XLA Ops:
  1.3 38.9 %step.1 = (bf16[16,24,512]{2,1,0:T(8,128)(2,1)S(1)}, bf16[64,512]{1,0:T(8,128)(2,1)S(1)}, bf16[4,24,512]{2,1,0:T(8,128)(2,1)S(1)}, bf16[16,512]{1,0:T(8,128)(2,1)S(1)}, bf16[16,32,256]{2,1,0:T(8,128)(2,1)S(1)}) custom-call(bf16[16,32,256]{2,1,0:T(8,128)(2,1)} %refs_0_.1, f32[4,256]{1,0:T(4,128)} %bitcast.11, s32[16,32]{1,0:T(8,128)} %refs_2_.1, ...), custom_call_target="tpu_custom_call" | custom-call | tf_op jit(solution)/shard_map/step/pallas_call | solution.py:540
  40.2 0.9 %last.1 = (bf16[16,24,512]{2,1,0:T(8,128)(2,1)}, bf16[16,32,256]{2,1,0:T(8,128)(2,1)}) custom-call(bf16[16,24,512]{2,1,0:T(8,128)(2,1)S(1)} %get-tuple-element.7.cyc_ref, bf16[64,512]{1,0:T(8,128)(2,1)S(1)} %get-tuple-element.8.west_ref, bf16[4,24,512]{2,1,0:T(8,128)(2,1)S(1)} %get-tuple-element.9.south_ref, bf16[16,512]{1,0:T(8,128)(2,1)S(1)} %get-tuple-element.10.sw_ref, ...), custom_call_target="tpu_custom_call" | custom-call | tf_op jit(solution)/shard_map/last/pallas_call | solution.py:525
